TPU v7x, 512 devices: a whole 4x4x16 slice. The times are simulated.
512 devices in a mesh: gx: 16 (over z_hi, y), gy: 32 (over z_lo, x, core).
Axes of the slice: x: 4, y: 4, z: 16 (z_hi: 4, z_lo: 4; z = z_hi * 4 + z_lo), core: 2. Of those that a mesh axis runs over, the one named last changes fastest.
Arguments:
- density: float32 [128, 512, 128], P('gx', 'gy'), may hold values from -3 to 3
- populations: float32 [19, 64, 64, 256], P(None, 'gx', 'gy'), may hold values from 0 to 0.6, as said below
Outputs:
- density_next: float32 [128, 512, 128], P('gx', 'gy')
- populations_next: float32 [19, 64, 64, 256], P(None, 'gx', 'gy')
Inputs may be any that keep to these rules, and one draw needn't show every extreme that they name: `populations`: each population is its lattice weight times a factor between 0.4 and 1.6.
All inputs are finite; a program needn't handle non-finite values.
Results may differ from a plain program's by a relative error of at most 0.00023.
Values sent between devices are 32-bit elements; how exact they have to be, the bound alone decides.
A program may use at most 64 MiB of HBM per device.

v0:
```python
import jax
import jax.numpy as jnp
from jax import lax
from jax.sharding import PartitionSpec as P

DENSITY_SUBSTEPS = 2


coupled_time_step = 0.0008
force_unit = 0.005
speed_unit = 2000.0
relax_time = 0.8
quench_depth = -0.25


def from_behind(value, axis, steps):
    count = lax.axis_size(axis)
    pairs = [(source, (source + steps) % count) for source in range(count)]
    return lax.ppermute(value, axis, pairs)


def padded(block, sides, width):
    for axis, dim in sides:
        count = lax.axis_size(axis)
        forward = [(i, i + 1) for i in range(count - 1)]
        forward.append((count - 1, 0))
        backward = [(target, source) for source, target in forward]
        low = lax.ppermute(
            lax.slice_in_dim(block, block.shape[dim] - width, None, axis=dim), axis, forward
        )
        high = lax.ppermute(lax.slice_in_dim(block, 0, width, axis=dim), axis, backward)
        block = jnp.concatenate([low, block, high], axis=dim)
    return block


def lattice():
    speeds = [
        (0, 0, 0),
        (1, 0, 0),
        (-1, 0, 0),
        (0, 1, 0),
        (0, -1, 0),
        (0, 0, 1),
        (0, 0, -1),
        (1, 1, 0),
        (-1, -1, 0),
        (1, -1, 0),
        (-1, 1, 0),
        (1, 0, 1),
        (-1, 0, -1),
        (1, 0, -1),
        (-1, 0, 1),
        (0, 1, 1),
        (0, -1, -1),
        (0, 1, -1),
        (0, -1, 1),
    ]
    weights = [1.0 / 3.0] + [1.0 / 18.0] * 6 + [1.0 / 36.0] * 12
    return (speeds, weights)


def laplace_ext(grid_field):
    center = grid_field[1:-1, 1:-1]
    running = -6.0 * center
    running = running + grid_field[:-2, 1:-1] + grid_field[2:, 1:-1]
    running = running + grid_field[1:-1, :-2] + grid_field[1:-1, 2:]
    running = running + jnp.roll(center, 1, 2) + jnp.roll(center, -1, 2)
    return running


def potential_ext(grid_field):
    first_lap = laplace_ext(grid_field)
    core_part = grid_field[2:-2, 2:-2]
    return (
        quench_depth * core_part
        + core_part
        + 2.0 * first_lap[1:-1, 1:-1]
        + laplace_ext(first_lap)
        + core_part * core_part * core_part
    )


def central_ext(grid_field, dimension):
    if dimension == 0:
        return (grid_field[2:, 1:-1] - grid_field[:-2, 1:-1]) * 0.5
    if dimension == 1:
        return (grid_field[1:-1, 2:] - grid_field[1:-1, :-2]) * 0.5
    center = grid_field[1:-1, 1:-1]
    return (jnp.roll(center, -1, 2) - jnp.roll(center, 1, 2)) * 0.5


def coarse_mean(grid_field):
    size_x, size_y, extent_along_z = grid_field.shape
    return grid_field.reshape(size_x // 2, 2, size_y // 2, 2, extent_along_z // 2, 2).mean(
        axis=(1, 3, 5)
    )


def collide(populations, coarse_force):
    speeds, weights = lattice()
    speed_table = jnp.array(speeds, jnp.float32)
    weight_table = jnp.array(weights, jnp.float32)[:, None, None, None]
    fluid_mass = jnp.sum(populations, axis=0)
    moment = jnp.einsum("qc,qxzy->cxzy", speed_table, populations, precision=lax.Precision.HIGHEST)
    flow_velocity = (moment + 0.5 * coarse_force) / fluid_mass
    speed_square = (
        flow_velocity[0] * flow_velocity[0]
        + flow_velocity[1] * flow_velocity[1]
        + flow_velocity[2] * flow_velocity[2]
    )
    force_velocity = (
        flow_velocity[0] * coarse_force[0]
        + flow_velocity[1] * coarse_force[1]
        + flow_velocity[2] * coarse_force[2]
    )
    column_x = speed_table[:, 0][:, None, None, None]
    column_y = speed_table[:, 1][:, None, None, None]
    column_z = speed_table[:, 2][:, None, None, None]
    projected = (
        column_x * flow_velocity[0] + column_y * flow_velocity[1] + column_z * flow_velocity[2]
    )
    force_along = (
        column_x * coarse_force[0] + column_y * coarse_force[1] + column_z * coarse_force[2]
    )
    balance = (
        weight_table
        * fluid_mass
        * (1.0 + 3.0 * projected + 4.5 * projected * projected - 1.5 * speed_square)
    )
    source_gain = 1.0 - 0.5 / relax_time
    relaxed = (
        populations
        - (populations - balance) / relax_time
        + source_gain
        * weight_table
        * (3.0 * (force_along - force_velocity) + 9.0 * projected * force_along)
    )
    return (relaxed, flow_velocity)


def propagate_moving(relaxed):
    speeds, weights = lattice()
    rising_x = [member for member in range(len(speeds)) if speeds[member][0] == 1]
    falling_x = [member for member in range(len(speeds)) if speeds[member][0] == -1]
    rising_z = [member for member in range(len(speeds)) if speeds[member][2] == 1]
    falling_z = [member for member in range(len(speeds)) if speeds[member][2] == -1]
    below_x = from_behind(jnp.stack([relaxed[member, -1:] for member in rising_x]), "gx", 1)
    above_x = from_behind(jnp.stack([relaxed[member, :1] for member in falling_x]), "gx", -1)
    moved_list = []
    for member in range(len(speeds)):
        plane_now = relaxed[member]
        if member in rising_x:
            plane_now = jnp.concatenate([below_x[rising_x.index(member)], plane_now[:-1]], axis=0)
        elif member in falling_x:
            plane_now = jnp.concatenate([plane_now[1:], above_x[falling_x.index(member)]], axis=0)
        moved_list.append(plane_now)
    below_z = from_behind(jnp.stack([moved_list[member][:, -1:] for member in rising_z]), "gy", 1)
    above_z = from_behind(jnp.stack([moved_list[member][:, :1] for member in falling_z]), "gy", -1)
    passed = []
    for member in range(len(speeds)):
        plane_now = moved_list[member]
        if member in rising_z:
            plane_now = jnp.concatenate(
                [below_z[rising_z.index(member)], plane_now[:, :-1]], axis=1
            )
        elif member in falling_z:
            plane_now = jnp.concatenate(
                [plane_now[:, 1:], above_z[falling_z.index(member)]], axis=1
            )
        passed.append(jnp.roll(plane_now, speeds[member][1], 2))
    return jnp.stack(passed)


def local(density, populations):
    size_x, size_y, extent_along_z = density.shape
    current = density
    fine_velocity = None
    populations_next = None
    for inner_substep in range(DENSITY_SUBSTEPS):
        extended = padded(current, (("gx", 0), ("gy", 1)), 3)
        potential = potential_ext(extended)
        nearby = extended[2:-2, 2:-2]
        interior = nearby[1:-1, 1:-1]
        if inner_substep == 0:
            pieces = []
            for dimension in range(3):
                pieces.append(
                    force_unit
                    * coarse_mean(-interior * central_ext(potential, dimension)).transpose(0, 2, 1)
                )
            coarse_force = lax.all_to_all(
                jnp.stack(pieces), "gy", split_axis=2, concat_axis=3, tiled=True
            )
            relaxed, flow_velocity = collide(populations, coarse_force)
            populations_next = propagate_moving(relaxed)
            returned = lax.all_to_all(
                speed_unit * flow_velocity, "gy", split_axis=3, concat_axis=2, tiled=True
            )
            returned = returned.transpose(0, 1, 3, 2)
            half_x, half_y, half_z = (returned.shape[1], returned.shape[2], returned.shape[3])
            fine_velocity = jnp.broadcast_to(
                returned[:, :, None, :, None, :, None], (3, half_x, 2, half_y, 2, half_z, 2)
            ).reshape(3, size_x, size_y, extent_along_z)
        advect = (
            fine_velocity[0] * central_ext(nearby, 0)
            + fine_velocity[1] * central_ext(nearby, 1)
            + fine_velocity[2] * central_ext(nearby, 2)
        )
        current = interior + coupled_time_step * (laplace_ext(potential) - advect)
    return (current, populations_next)


def solution(mesh):
    return jax.shard_map(
        local,
        mesh=mesh,
        in_specs=(P("gx", "gy", None), P(None, "gx", "gy", None)),
        out_specs=(P("gx", "gy", None), P(None, "gx", "gy", None)),
        check_vma=False,
    )
```

profile of v0, /device:TPU:103, one launch (start us, length us, event | category | flops | bytes accessed | tf_op | source)
XLA Modules:
  0.0 167.7 jit_solution(1804815233321957827)
XLA Ops:
  0.6 0.8 fusion.107
  1.4 3.2 %collective-permute-start = (f32[3,16,128]{2,1,0:T(8,128)S(1)}, f32[3,16,128]{2,1,0:T(8,128)S(1)}, u32[]{:S(2)}, u32[]{:S(2)}) collective-permute-start(f32[3,16,128]{2,1,0:T(8,128)S(1)} %get-tuple-element.81), channel_id=1, source_target_pairs={{0,32},{32,64},{64,96},{96,128},{128,160},{160,192},{192,224},{224... | collective-permute-start | bytes 73736 | tf_op jit(solution)/shard_map/ppermute | solution.py:28
  4.7 10.9 %collective-permute-start.1 = (f32[3,16,128]{2,1,0:T(8,128)S(1)}, f32[3,16,128]{2,1,0:T(8,128)S(1)}, u32[]{:S(2)}, u32[]{:S(2)}) collective-permute-start(f32[3,16,128]{2,1,0:T(8,128)S(1)} %get-tuple-element.80), channel_id=1, source_target_pairs={{32,0},{64,32},{96,64},{128,96},{160,128},{192,160},{224,192},{256... | collective-permute-start | bytes 73736 | tf_op jit(solution)/shard_map/ppermute | solution.py:31
  15.6 1.2 fusion
  16.8 0.8 constant_dynamic-update-slice_fusion.1
  17.7 2.9 %collective-permute-start.3 = (f32[14,3,128]{2,1,0:T(4,128)S(1)}, f32[14,3,128]{2,1,0:T(4,128)S(1)}, u32[]{:S(2)}, u32[]{:S(2)}) collective-permute-start(f32[14,3,128]{2,1,0:T(4,128)S(1)} %get-tuple-element.65), channel_id=1, source_target_pairs={{1,0},{2,1},{3,2},{4,3},{5,4},{6,5},{7,6},{8,7},{9,8},{10,9},{11,1... | collective-permute-start | bytes 64520 | tf_op jit(solution)/shard_map/ppermute | solution.py:31
  20.5 6.6 %collective-permute-start.2 = (f32[14,3,128]{2,1,0:T(4,128)S(1)}, f32[14,3,128]{2,1,0:T(4,128)S(1)}, u32[]{:S(2)}, u32[]{:S(2)}) collective-permute-start(f32[14,3,128]{2,1,0:T(4,128)S(1)} %get-tuple-element.64), channel_id=1, source_target_pairs={{0,1},{1,2},{2,3},{3,4},{4,5},{5,6},{6,7},{7,8},{8,9},{9,10},{10,1... | collective-permute-start | bytes 64520 | tf_op jit(solution)/shard_map/ppermute | solution.py:28
  27.2 1.0 fusion.105
  29.2 5.5 %reshape.61 = f32[4,2,8,2,64,2]{5,4,3,2,1,0:T(8,128)} reshape(f32[8,16,128]{2,1,0:T(8,128)S(1)} %get-tuple-element.79) | data formatting | bytes 131072 | tf_op jit(solution)/shard_map/reshape | solution.py:94
  34.8 5.6 %reshape.60 = f32[4,2,8,2,64,2]{5,4,3,2,1,0:T(8,128)} reshape(f32[8,16,128]{2,1,0:T(8,128)S(1)} %get-tuple-element.8) | data formatting | bytes 131072 | tf_op jit(solution)/shard_map/reshape | solution.py:94
  40.4 2.5 %reduce_sum.38 = f32[4,8,64]{2,1,0:T(8,128)S(1)} reduce(f32[4,2,8,2,64,2]{5,4,3,2,1,0:T(8,128)} %reshape.61, f32[]{:T(128)} %constant.9.clone.1), dimensions={1,3,5}, to_apply=%region_2.3 | reduce | flops 14336 | bytes 73732 | tf_op jit(solution)/shard_map/reduce_sum | solution.py:94
  42.9 2.6 %reduce_sum.37 = f32[4,8,64]{2,1,0:T(8,128)S(1)} reduce(f32[4,2,8,2,64,2]{5,4,3,2,1,0:T(8,128)} %reshape.60, f32[]{:T(128)} %constant.9.clone.1), dimensions={1,3,5}, to_apply=%region_1.2 | reduce | flops 14336 | bytes 73732 | tf_op jit(solution)/shard_map/reduce_sum | solution.py:94
  45.5 5.5 %reshape.59 = f32[4,2,8,2,64,2]{5,4,3,2,1,0:T(8,128)} reshape(f32[8,16,128]{2,1,0:T(8,128)S(1)} %get-tuple-element.7) | data formatting | bytes 131072 | tf_op jit(solution)/shard_map/reshape | solution.py:94
  51.1 2.6 %reduce_sum.36 = f32[4,8,64]{2,1,0:T(8,128)S(1)} reduce(f32[4,2,8,2,64,2]{5,4,3,2,1,0:T(8,128)} %reshape.59, f32[]{:T(128)} %constant.9.clone.1), dimensions={1,3,5}, to_apply=%region_0.1 | reduce | flops 14336 | bytes 73732 | tf_op jit(solution)/shard_map/reduce_sum | solution.py:94
  53.9 1.0 reshape.67
  54.9 9.9 %all-to-all-start = ((f32[32,1,192]{2,1,0:T(1,128)}), f32[32,1,192]{2,1,0:T(1,128)S(1)}, u32[]{:S(2)}, u32[]{:S(2)}) async-start(f32[32,1,192]{2,1,0:T(1,128)} %reshape.67), calls=%async_computation | async-start | bytes 65536 | tf_op jit(solution)/shard_map/all_to_all | solution.py:191
  64.9 3.0 %all-to-all-done = f32[32,1,192]{2,1,0:T(1,128)S(1)} async-done(((f32[32,1,192]{2,1,0:T(1,128)}), f32[32,1,192]{2,1,0:T(1,128)S(1)}, u32[]{:S(2)}, u32[]{:S(2)}) %all-to-all-start) | async-done | bytes 24608 | tf_op jit(solution)/shard_map/all_to_all | solution.py:191
  67.9 0.5 broadcast.87
  68.5 0.7 reduce
  69.2 0.3 reshape.68
  70.5 0.2 reshape.63
  71.6 0.7 multiply_add_fusion.2
  72.4 1.9 %collective-permute-start.8 = (f32[5,1,2,256]{3,2,1,0:T(2,128)S(1)}, f32[5,1,2,256]{3,2,1,0:T(2,128)S(1)}, u32[]{:S(2)}, u32[]{:S(2)}) collective-permute-start(f32[5,1,2,256]{3,2,1,0:T(2,128)S(1)} %get-tuple-element.37), channel_id=1, source_target_pairs={{0,32},{32,64},{64,96},{96,128},{128,160},{160,192},{192,224},{224... | collective-permute-start | bytes 30728 | tf_op jit(solution)/shard_map/ppermute | solution.py:19
  74.5 0.6 copy.101
  75.1 1.8 %reshape.69 = f32[32,1,192]{2,1,0:T(1,128)} reshape(f32[256,3,2,4]{3,2,1,0:T(2,128)S(1)} %bitcast.253) | data formatting | bytes 49152
  76.8 8.5 %all-to-all-start.1 = ((f32[32,1,192]{2,1,0:T(1,128)}), f32[32,1,192]{2,1,0:T(1,128)S(1)}, u32[]{:S(2)}, u32[]{:S(2)}) async-start(f32[32,1,192]{2,1,0:T(1,128)} %reshape.69), calls=%async_computation.1 | async-start | bytes 65536 | tf_op jit(solution)/shard_map/all_to_all | solution.py:196
  85.3 9.7 %collective-permute-start.9 = (f32[5,1,2,256]{3,2,1,0:T(2,128)S(1)}, f32[5,1,2,256]{3,2,1,0:T(2,128)S(1)}, u32[]{:S(2)}, u32[]{:S(2)}) collective-permute-start(f32[5,1,2,256]{3,2,1,0:T(2,128)S(1)} %get-tuple-element.36), channel_id=1, source_target_pairs={{0,480},{32,0},{64,32},{96,64},{128,96},{160,128},{192,160},{224,1... | collective-permute-start | bytes 30728 | tf_op jit(solution)/shard_map/ppermute | solution.py:19
  95.1 0.6 collective-permute-done.9
  95.8 2.9 %collective-permute-start.10 = (f32[5,4,1,256]{3,2,1,0:T(1,128)S(1)}, f32[5,4,1,256]{3,2,1,0:T(1,128)S(1)}, u32[]{:S(2)}, u32[]{:S(2)}) collective-permute-start(f32[5,4,1,256]{3,2,1,0:T(1,128)S(1)} %constant_dynamic-update-slice_fusion.13), channel_id=1, source_target_pairs={{0,1},{1,2},{2,3},{3,4},{4,5},{5,6},{6,7},{7,8},{8,9},{9,10},{10,1... | collective-permute-start | bytes 61448 | tf_op jit(solution)/shard_map/ppermute | solution.py:19
  98.8 2.3 %collective-permute-start.11 = (f32[5,4,1,256]{3,2,1,0:T(1,128)S(1)}, f32[5,4,1,256]{3,2,1,0:T(1,128)S(1)}, u32[]{:S(2)}, u32[]{:S(2)}) collective-permute-start(f32[5,4,1,256]{3,2,1,0:T(1,128)S(1)} %constant_dynamic-update-slice_fusion.18), channel_id=1, source_target_pairs={{0,31},{1,0},{2,1},{3,2},{4,3},{5,4},{6,5},{7,6},{8,7},{9,8},{10,9... | collective-permute-start | bytes 61448 | tf_op jit(solution)/shard_map/ppermute | solution.py:19
  101.7 6.1 %collective-permute-done.11 = f32[5,4,1,256]{3,2,1,0:T(1,128)S(1)} collective-permute-done((f32[5,4,1,256]{3,2,1,0:T(1,128)S(1)}, f32[5,4,1,256]{3,2,1,0:T(1,128)S(1)}, u32[]{:S(2)}, u32[]{:S(2)}) %collective-permute-start.11) | collective-permute-done | bytes 20512 | tf_op jit(solution)/shard_map/ppermute | solution.py:19
  109.0 0.7 reduce.1
  109.7 1.2 reshape.70
  110.9 1.6 copy.125
  112.4 0.3 copy.103
  112.9 2.6 %broadcast_in_dim.23 = f32[4,2,8,2,64,2]{5,4,3,2,1,0:T(8,128)} broadcast(f32[4,8,64]{2,1,0:T(8,128)S(1)} %copy.105), dimensions={0,2,4} | broadcast | bytes 73728 | tf_op jit(solution)/shard_map/broadcast_in_dim | solution.py:201
  115.4 4.0 %broadcast_in_dim.24 = f32[8,16,128]{2,1,0:T(8,128)S(1)} reshape(f32[4,2,8,2,64,2]{5,4,3,2,1,0:T(8,128)} %broadcast_in_dim.23) | data formatting | bytes 131072 | tf_op jit(solution)/shard_map/broadcast_in_dim | solution.py:201
  119.5 2.6 %broadcast_in_dim.21 = f32[4,2,8,2,64,2]{5,4,3,2,1,0:T(8,128)} broadcast(f32[4,8,64]{2,1,0:T(8,128)S(1)} %copy.104), dimensions={0,2,4} | broadcast | bytes 73728 | tf_op jit(solution)/shard_map/broadcast_in_dim | solution.py:201
  122.1 4.0 %broadcast_in_dim.22 = f32[8,16,128]{2,1,0:T(8,128)S(1)} reshape(f32[4,2,8,2,64,2]{5,4,3,2,1,0:T(8,128)} %broadcast_in_dim.21) | data formatting | bytes 131072 | tf_op jit(solution)/shard_map/broadcast_in_dim | solution.py:201
  126.2 2.6 %broadcast_in_dim.25 = f32[4,2,8,2,64,2]{5,4,3,2,1,0:T(8,128)} broadcast(f32[4,8,64]{2,1,0:T(8,128)S(1)} %copy.106), dimensions={0,2,4} | broadcast | bytes 73728 | tf_op jit(solution)/shard_map/broadcast_in_dim | solution.py:201
  128.8 4.0 %broadcast_in_dim.26 = f32[8,16,128]{2,1,0:T(8,128)S(1)} reshape(f32[4,2,8,2,64,2]{5,4,3,2,1,0:T(8,128)} %broadcast_in_dim.25) | data formatting | bytes 131072 | tf_op jit(solution)/shard_map/broadcast_in_dim | solution.py:201
  133.0 9.9 %collective-permute-start.5 = (f32[3,16,128]{2,1,0:T(8,128)S(1)}, f32[3,16,128]{2,1,0:T(8,128)S(1)}, u32[]{:S(2)}, u32[]{:S(2)}) collective-permute-start(f32[3,16,128]{2,1,0:T(8,128)S(1)} %get-tuple-element.74), channel_id=1, source_target_pairs={{32,0},{64,32},{96,64},{128,96},{160,128},{192,160},{224,192},{256... | collective-permute-start | bytes 73736 | tf_op jit(solution)/shard_map/ppermute | solution.py:31
  142.9 1.9 %collective-permute-start.4 = (f32[3,16,128]{2,1,0:T(8,128)S(1)}, f32[3,16,128]{2,1,0:T(8,128)S(1)}, u32[]{:S(2)}, u32[]{:S(2)}) collective-permute-start(f32[3,16,128]{2,1,0:T(8,128)S(1)} %get-tuple-element.73), channel_id=1, source_target_pairs={{0,32},{32,64},{64,96},{96,128},{128,160},{160,192},{192,224},{224... | collective-permute-start | bytes 73736 | tf_op jit(solution)/shard_map/ppermute | solution.py:28
  144.9 8.7 %collective-permute-done.4 = f32[3,16,128]{2,1,0:T(8,128)S(1)} collective-permute-done((f32[3,16,128]{2,1,0:T(8,128)S(1)}, f32[3,16,128]{2,1,0:T(8,128)S(1)}, u32[]{:S(2)}, u32[]{:S(2)}) %collective-permute-start.4) | collective-permute-done | bytes 24608 | tf_op jit(solution)/shard_map/ppermute | solution.py:28
  153.7 3.2 %collective-permute-start.6 = (f32[14,3,128]{2,1,0:T(4,128)S(1)}, f32[14,3,128]{2,1,0:T(4,128)S(1)}, u32[]{:S(2)}, u32[]{:S(2)}) collective-permute-start(f32[14,3,128]{2,1,0:T(4,128)S(1)} %get-tuple-element.63), channel_id=1, source_target_pairs={{0,1},{1,2},{2,3},{3,4},{4,5},{5,6},{6,7},{7,8},{8,9},{9,10},{10,1... | collective-permute-start | bytes 64520 | tf_op jit(solution)/shard_map/ppermute | solution.py:28
  156.9 1.9 %collective-permute-start.7 = (f32[14,3,128]{2,1,0:T(4,128)S(1)}, f32[14,3,128]{2,1,0:T(4,128)S(1)}, u32[]{:S(2)}, u32[]{:S(2)}) collective-permute-start(f32[14,3,128]{2,1,0:T(4,128)S(1)} %get-tuple-element.62), channel_id=1, source_target_pairs={{1,0},{2,1},{3,2},{4,3},{5,4},{6,5},{7,6},{8,7},{9,8},{10,9},{11,1... | collective-permute-start | bytes 64520 | tf_op jit(solution)/shard_map/ppermute | solution.py:31
  158.9 7.1 %collective-permute-done.7 = f32[14,3,128]{2,1,0:T(4,128)S(1)} collective-permute-done((f32[14,3,128]{2,1,0:T(4,128)S(1)}, f32[14,3,128]{2,1,0:T(4,128)S(1)}, u32[]{:S(2)}, u32[]{:S(2)}) %collective-permute-start.7) | collective-permute-done | bytes 21536 | tf_op jit(solution)/shard_map/ppermute | solution.py:31
  166.9 0.8 fusion.27
  (142 shorter events, 6.6 us)
Async XLA Ops:
  0.6 28.5 %copy-start = (f32[8,16,128]{2,1,0:T(8,128)S(1)}, f32[8,16,128]{2,1,0:T(8,128)}, u32[]{:S(2)}) copy-start(f32[8,16,128]{2,1,0:T(8,128)} %param.4) | copy-start | bytes 196612
  1.4 15.3 %collective-permute-start = (f32[3,16,128]{2,1,0:T(8,128)S(1)}, f32[3,16,128]{2,1,0:T(8,128)S(1)}, u32[]{:S(2)}, u32[]{:S(2)}) collective-permute-start(f32[3,16,128]{2,1,0:T(8,128)S(1)} %get-tuple-element.81), channel_id=1, source_target_pairs={{0,32},{32,64},{64,96},{96,128},{128,160},{160,192},{192,224},{224... | collective-permute-start | bytes 73736 | tf_op jit(solution)/shard_map/ppermute | solution.py:28
  4.7 13.0 %collective-permute-start.1 = (f32[3,16,128]{2,1,0:T(8,128)S(1)}, f32[3,16,128]{2,1,0:T(8,128)S(1)}, u32[]{:S(2)}, u32[]{:S(2)}) collective-permute-start(f32[3,16,128]{2,1,0:T(8,128)S(1)} %get-tuple-element.80), channel_id=1, source_target_pairs={{32,0},{64,32},{96,64},{128,96},{160,128},{192,160},{224,192},{256... | collective-permute-start | bytes 73736 | tf_op jit(solution)/shard_map/ppermute | solution.py:31
  17.7 10.5 %collective-permute-start.3 = (f32[14,3,128]{2,1,0:T(4,128)S(1)}, f32[14,3,128]{2,1,0:T(4,128)S(1)}, u32[]{:S(2)}, u32[]{:S(2)}) collective-permute-start(f32[14,3,128]{2,1,0:T(4,128)S(1)} %get-tuple-element.65), channel_id=1, source_target_pairs={{1,0},{2,1},{3,2},{4,3},{5,4},{6,5},{7,6},{8,7},{9,8},{10,9},{11,1... | collective-permute-start | bytes 64520 | tf_op jit(solution)/shard_map/ppermute | solution.py:31
  20.5 7.6 %collective-permute-start.2 = (f32[14,3,128]{2,1,0:T(4,128)S(1)}, f32[14,3,128]{2,1,0:T(4,128)S(1)}, u32[]{:S(2)}, u32[]{:S(2)}) collective-permute-start(f32[14,3,128]{2,1,0:T(4,128)S(1)} %get-tuple-element.64), channel_id=1, source_target_pairs={{0,1},{1,2},{2,3},{3,4},{4,5},{5,6},{6,7},{7,8},{8,9},{9,10},{10,1... | collective-permute-start | bytes 64520 | tf_op jit(solution)/shard_map/ppermute | solution.py:28
  45.5 19.3 %copy-start.1 = (f32[19,4,2,256]{3,2,1,0:T(2,128)S(1)}, f32[19,4,2,256]{3,2,1,0:T(2,128)}, u32[]{:S(2)}) copy-start(f32[19,4,2,256]{3,2,1,0:T(2,128)} %param.5) | copy-start | bytes 466948
  51.0 20.5 %copy-start.2 = (f32[19]{0:T(128)S(1)}, f32[19]{0:T(128)}, u32[]{:S(2)}) copy-start(f32[19]{0:T(128)} %constant.55) | copy-start | bytes 232
  51.0 20.5 %copy-start.3 = (f32[19]{0:T(128)S(1)}, f32[19]{0:T(128)}, u32[]{:S(2)}) copy-start(f32[19]{0:T(128)} %constant.46.clone) | copy-start | bytes 232
  51.0 20.5 %copy-start.4 = (f32[19]{0:T(128)S(1)}, f32[19]{0:T(128)}, u32[]{:S(2)}) copy-start(f32[19]{0:T(128)} %constant.54) | copy-start | bytes 232
  51.0 20.6 %copy-start.5 = (f32[19]{0:T(128)S(1)}, f32[19]{0:T(128)}, u32[]{:S(2)}) copy-start(f32[19]{0:T(128)} %constant.52) | copy-start | bytes 232
  51.0 20.6 %copy-start.6 = (f32[19]{0:T(128)S(1)}, f32[19]{0:T(128)}, u32[]{:S(2)}) copy-start(f32[19]{0:T(128)} %constant.50) | copy-start | bytes 232
  54.9 13.1 %all-to-all-start = ((f32[32,1,192]{2,1,0:T(1,128)}), f32[32,1,192]{2,1,0:T(1,128)S(1)}, u32[]{:S(2)}, u32[]{:S(2)}) async-start(f32[32,1,192]{2,1,0:T(1,128)} %reshape.67), calls=%async_computation | async-start | bytes 65536 | tf_op jit(solution)/shard_map/all_to_all | solution.py:191
  72.4 22.7 %collective-permute-start.8 = (f32[5,1,2,256]{3,2,1,0:T(2,128)S(1)}, f32[5,1,2,256]{3,2,1,0:T(2,128)S(1)}, u32[]{:S(2)}, u32[]{:S(2)}) collective-permute-start(f32[5,1,2,256]{3,2,1,0:T(2,128)S(1)} %get-tuple-element.37), channel_id=1, source_target_pairs={{0,32},{32,64},{64,96},{96,128},{128,160},{160,192},{192,224},{224... | collective-permute-start | bytes 30728 | tf_op jit(solution)/shard_map/ppermute | solution.py:19
  76.8 32.1 %all-to-all-start.1 = ((f32[32,1,192]{2,1,0:T(1,128)}), f32[32,1,192]{2,1,0:T(1,128)S(1)}, u32[]{:S(2)}, u32[]{:S(2)}) async-start(f32[32,1,192]{2,1,0:T(1,128)} %reshape.69), calls=%async_computation.1 | async-start | bytes 65536 | tf_op jit(solution)/shard_map/all_to_all | solution.py:196
  85.3 10.5 %collective-permute-start.9 = (f32[5,1,2,256]{3,2,1,0:T(2,128)S(1)}, f32[5,1,2,256]{3,2,1,0:T(2,128)S(1)}, u32[]{:S(2)}, u32[]{:S(2)}) collective-permute-start(f32[5,1,2,256]{3,2,1,0:T(2,128)S(1)} %get-tuple-element.36), channel_id=1, source_target_pairs={{0,480},{32,0},{64,32},{96,64},{128,96},{160,128},{192,160},{224,1... | collective-permute-start | bytes 30728 | tf_op jit(solution)/shard_map/ppermute | solution.py:19
  95.8 5.8 %collective-permute-start.10 = (f32[5,4,1,256]{3,2,1,0:T(1,128)S(1)}, f32[5,4,1,256]{3,2,1,0:T(1,128)S(1)}, u32[]{:S(2)}, u32[]{:S(2)}) collective-permute-start(f32[5,4,1,256]{3,2,1,0:T(1,128)S(1)} %constant_dynamic-update-slice_fusion.13), channel_id=1, source_target_pairs={{0,1},{1,2},{2,3},{3,4},{4,5},{5,6},{6,7},{7,8},{8,9},{9,10},{10,1... | collective-permute-start | bytes 61448 | tf_op jit(solution)/shard_map/ppermute | solution.py:19
  98.8 9.0 %collective-permute-start.11 = (f32[5,4,1,256]{3,2,1,0:T(1,128)S(1)}, f32[5,4,1,256]{3,2,1,0:T(1,128)S(1)}, u32[]{:S(2)}, u32[]{:S(2)}) collective-permute-start(f32[5,4,1,256]{3,2,1,0:T(1,128)S(1)} %constant_dynamic-update-slice_fusion.18), channel_id=1, source_target_pairs={{0,31},{1,0},{2,1},{3,2},{4,3},{5,4},{6,5},{7,6},{8,7},{9,8},{10,9... | collective-permute-start | bytes 61448 | tf_op jit(solution)/shard_map/ppermute | solution.py:19
  109.0 10.5 %copy-start.7 = (f32[19,4,2,256]{3,2,1,0:T(2,128)}, f32[19,4,2,256]{3,2,1,0:T(2,128)S(1)}, u32[]{:S(2)}) copy-start(f32[19,4,2,256]{3,2,1,0:T(2,128)S(1)} %constant_dynamic-update-slice_fusion.23) | copy-start | bytes 466948
  133.0 12.0 %collective-permute-start.5 = (f32[3,16,128]{2,1,0:T(8,128)S(1)}, f32[3,16,128]{2,1,0:T(8,128)S(1)}, u32[]{:S(2)}, u32[]{:S(2)}) collective-permute-start(f32[3,16,128]{2,1,0:T(8,128)S(1)} %get-tuple-element.74), channel_id=1, source_target_pairs={{32,0},{64,32},{96,64},{128,96},{160,128},{192,160},{224,192},{256... | collective-permute-start | bytes 73736 | tf_op jit(solution)/shard_map/ppermute | solution.py:31
  142.9 10.7 %collective-permute-start.4 = (f32[3,16,128]{2,1,0:T(8,128)S(1)}, f32[3,16,128]{2,1,0:T(8,128)S(1)}, u32[]{:S(2)}, u32[]{:S(2)}) collective-permute-start(f32[3,16,128]{2,1,0:T(8,128)S(1)} %get-tuple-element.73), channel_id=1, source_target_pairs={{0,32},{32,64},{64,96},{96,128},{128,160},{160,192},{192,224},{224... | collective-permute-start | bytes 73736 | tf_op jit(solution)/shard_map/ppermute | solution.py:28
  153.7 5.2 %collective-permute-start.6 = (f32[14,3,128]{2,1,0:T(4,128)S(1)}, f32[14,3,128]{2,1,0:T(4,128)S(1)}, u32[]{:S(2)}, u32[]{:S(2)}) collective-permute-start(f32[14,3,128]{2,1,0:T(4,128)S(1)} %get-tuple-element.63), channel_id=1, source_target_pairs={{0,1},{1,2},{2,3},{3,4},{4,5},{5,6},{6,7},{7,8},{8,9},{9,10},{10,1... | collective-permute-start | bytes 64520 | tf_op jit(solution)/shard_map/ppermute | solution.py:28
  156.9 9.1 %collective-permute-start.7 = (f32[14,3,128]{2,1,0:T(4,128)S(1)}, f32[14,3,128]{2,1,0:T(4,128)S(1)}, u32[]{:S(2)}, u32[]{:S(2)}) collective-permute-start(f32[14,3,128]{2,1,0:T(4,128)S(1)} %get-tuple-element.62), channel_id=1, source_target_pairs={{1,0},{2,1},{3,2},{4,3},{5,4},{6,5},{7,6},{8,7},{9,8},{10,9},{11,1... | collective-permute-start | bytes 64520 | tf_op jit(solution)/shard_map/ppermute | solution.py:31
where the time goes:
time: 169 us; the launch traced here: 168 us
  starting transfers between devices  75.7 us (45%)
  local copies, waits for them, and re-layouts  50.4 us (30%)
  waiting for transfers between devices  25.6 us (15%)
  other arithmetic  13.3 us (8%)
    ppermute x4, starting transfers between devices, padded(): lax.ppermute(lax.slice_in_dim(block, 0, width, axis=dim), axis, backward)  25.6 us
    broadcast_in_dim x6, local copies, waits for them, and re-layouts, local(): jnp.broadcast_to(returned[:, :, None, :, None, :, None], (3, half_x, 2, h...  19.8 us
    ppermute x4, starting transfers between devices, from_behind(): return lax.ppermute(value, axis, pairs)  16.8 us
    reshape x3, local copies, waits for them, and re-layouts, coarse_mean(): grid_field.reshape(size_x // 2, 2, size_y // 2, 2, extent_along_z // 2, 2)  16.7 us
    ppermute x4, starting transfers between devices, padded(): lax.ppermute(lax.slice_in_dim(block, block.shape[dim] - width, None, axis...  14.9 us
    all_to_all x1, starting transfers between devices, local(): lax.all_to_all(jnp.stack(pieces), 'gy', split_axis=2, concat_axis=3, tile...  9.87 us
    ppermute x4, waiting for transfers between devices, padded(): lax.ppermute(lax.slice_in_dim(block, block.shape[dim] - width, None, axis...  8.74 us
    all_to_all x1, starting transfers between devices, local(): lax.all_to_all(speed_unit * flow_velocity, 'gy', split_axis=3, concat_axi...  8.45 us
  transfers between devices with their start and end apart: 14, of which 5 were waited for; matrix products, arithmetic and copies ran while one was open for 5% of the time, Pallas kernels for 0%

commit v1 on v0

v1 whole, which is shorter than its diff:
```python
import jax
import jax.numpy as jnp
from jax import lax
from jax.experimental import pallas as pl
from jax.experimental.pallas import tpu as pltpu
from jax.sharding import PartitionSpec as P

MESH = pl.DeviceIdType.MESH
EXACT = lax.Precision.HIGHEST
F32 = jnp.float32

TIME_STEP = 0.0008
FORCE_UNIT = 0.005
SPEED_UNIT = 2000.0
RELAX_TIME = 0.8
QUENCH = -0.25

SPEEDS = [
    (0, 0, 0),
    (1, 0, 0), (-1, 0, 0), (0, 1, 0), (0, -1, 0), (0, 0, 1), (0, 0, -1),
    (1, 1, 0), (-1, -1, 0), (1, -1, 0), (-1, 1, 0),
    (1, 0, 1), (-1, 0, -1), (1, 0, -1), (-1, 0, 1),
    (0, 1, 1), (0, -1, -1), (0, 1, -1), (0, -1, 1),
]
WEIGHTS = [1.0 / 3.0] + [1.0 / 18.0] * 6 + [1.0 / 36.0] * 12

ORDER = [13, 1, 7, 9, 11, 5, 15, 18, 14, 2, 8, 10, 12, 6, 16, 17, 13, 0, 3, 4]
RISE_X, RISE_Z, FALL_X, FALL_Z = 0, 4, 8, 12
SLOT = {}
for _place, _member in enumerate(ORDER):
    SLOT.setdefault(_member, _place)
MASS = 20
FIELDS = 24


def dot_t(a, b):
    return lax.dot_general(
        a, b, (((1,), (1,)), ((), ())), precision=EXACT, preferred_element_type=F32
    )


def t_dot(a, b):
    return lax.dot_general(
        a, b, (((0,), (0,)), ((), ())), precision=EXACT, preferred_element_type=F32
    )


def iota(shape, dim):
    return lax.broadcasted_iota(jnp.int32, shape, dim)


def kernel(
    nx, n, dens_hbm, pops_hbm, dens_out, pops_out,
    E, E1, L1, PT, FA, FB, SP, SF, RF, SM, RM, MQ, NB, PV, EP, XS, XR, ZS, ZR, FR, RS, OP, OD,
    dsem, psem, odsem, opsem, xs_s, xs_r, ys_s, ys_r, cs_s, cs_r, x2_s, x2_r, y2_s, y2_r,
    c2_s, c2_r, px_s, px_r, pz_s, pz_r, ms_s, ms_r, fs_s, fs_r,
):
    L = 4 * n
    gx = lax.axis_index("gx")
    gy = lax.axis_index("gy")
    xu, xd = lax.rem(gx + 1, nx), lax.rem(gx + nx - 1, nx)
    yu, yd = lax.rem(gy + 1, n), lax.rem(gy + n - 1, n)
    UPX, DNX = {"gx": xu, "gy": gy}, {"gx": xd, "gy": gy}
    UPY, DNY = {"gx": gx, "gy": yu}, {"gx": gx, "gy": yd}

    barrier = pltpu.get_barrier_semaphore()
    for where in (UPX, DNX):
        pl.semaphore_signal(barrier, inc=1, device_id=where, device_id_type=MESH)

    @pl.loop(1, n)
    def _(k):
        pl.semaphore_signal(
            barrier, inc=1, device_id={"gx": gx, "gy": lax.rem(gy + k, n)}, device_id_type=MESH
        )

    dens_in = pltpu.make_async_copy(dens_hbm, E.at[pl.ds(5, 8), pl.ds(8, 16)], dsem)
    dens_in.start()
    pops_in = pltpu.make_async_copy(pops_hbm, PV, psem)
    pops_in.start()

    def remote(src, dst, send, recv, where):
        return pltpu.make_async_remote_copy(
            src_ref=src, dst_ref=dst, send_sem=send, recv_sem=recv, device_id=where,
            device_id_type=MESH,
        )

    lane = iota((1, L), 1)

    pops_in.wait()
    for h in range(2):
        for place, member in enumerate(ORDER):
            for x in range(4):
                EP[h, place, pl.ds(x * 4 + 5, 2), :] = PV[member, x, :, pl.ds(h * L, L)]
        total = jnp.zeros((24, L), F32)
        moment = [jnp.zeros((24, L), F32) for _ in range(3)]
        for member in range(19):
            value = EP[h, SLOT[member]]
            total = total + value
            for c in range(3):
                if SPEEDS[member][c] == 1:
                    moment[c] = moment[c] + value
                elif SPEEDS[member][c] == -1:
                    moment[c] = moment[c] - value
        EP[h, MASS] = total
        for c in range(3):
            EP[h, MASS + 1 + c] = moment[c]

    for way, (first, row) in enumerate(((RISE_X, 17), (FALL_X, 5))):
        for f in range(9):
            place = first + f if f < 5 else MASS + f - 5
            for h in range(2):
                XS[way, f * 2 + h] = EP[h, place, pl.ds(row, 2), :]

    spread = [
        (iota((n, L), 1) + h * L) // 8 == iota((n, L), 0) for h in range(2)
    ]
    spread = [jnp.where(s, 1.0, 0.0).astype(F32) for s in spread]
    for zl in range(2):
        result = None
        for h in range(2):
            for c in range(4):
                NB[h, pl.ds(c * 4, 4), :] = EP[h, MASS + c, pl.ds(5 + zl, 4, stride=4), :]
            block = NB[h]
            tiles = jnp.concatenate(
                [jnp.where(lax.rem(lane, 8) == y, block, 0.0) for y in range(8)], axis=0
            )
            part = dot_t(spread[h], tiles)
            result = part if result is None else result + part
        SM[pl.ds(zl, n, stride=8), :] = result

    dens_in.wait()
    pl.semaphore_wait(barrier, n + 1)

    def x_pair(buf, width, size, send, recv):
        lo = width
        return [
            remote(buf.at[pl.ds(lo + 8 - size, size), pl.ds(8, 16)],
                   buf.at[pl.ds(lo - size, size), pl.ds(8, 16)], send.at[0], recv.at[0], UPX),
            remote(buf.at[pl.ds(lo, size), pl.ds(8, 16)],
                   buf.at[pl.ds(lo + 8, size), pl.ds(8, 16)], send.at[1], recv.at[1], DNX),
        ]

    def y_pair(buf, x0, size, send, recv, k):
        return [
            remote(buf.at[pl.ds(x0, size), pl.ds(21, 3)],
                   buf.at[pl.ds(x0, size), pl.ds(5, 3)], send.at[k], recv.at[k], UPY),
            remote(buf.at[pl.ds(x0, size), pl.ds(8, 3)],
                   buf.at[pl.ds(x0, size), pl.ds(24, 3)], send.at[k + 1], recv.at[k + 1], DNY),
        ]

    halo_x = x_pair(E, 5, 5, xs_s, xs_r)
    halo_y = y_pair(E, 5, 8, ys_s, ys_r, 0)
    for copy in halo_x + halo_y:
        copy.start()

    def moment_copy(to, sem_to, slot):
        return remote(
            SM.at[pl.ds(pl.multiple_of(to * 8, 8), 2)],
            RM.at[pl.ds(pl.multiple_of(slot * 8, 8), 2)],
            ms_s.at[sem_to], ms_r.at[slot], {"gx": gx, "gy": to},
        )

    def force_copy(to, sem_to, slot):
        return remote(
            SF.at[pl.ds(pl.multiple_of(to * 8, 8), 5)],
            RF.at[pl.ds(pl.multiple_of(slot * 8, 8), 5)],
            fs_s.at[sem_to], fs_r.at[slot], {"gx": gx, "gy": to},
        )

    @pl.loop(1, n)
    def _(k):
        to = lax.rem(gy + k, n)
        moment_copy(to, to, gy).start()

    face_x = [
        remote(XS.at[0], XR.at[0], px_s.at[0], px_r.at[0], UPX),
        remote(XS.at[1], XR.at[1], px_s.at[1], px_r.at[1], DNX),
    ]
    for copy in face_x:
        copy.start()

    corners = []
    for way in range(2):
        halo_x[way].wait_recv()
        for copy in y_pair(E, 1 if way == 0 else 13, 4, cs_s, cs_r, 2 * way):
            copy.start()
            corners.append(copy)

    for way in range(2):
        face_x[way].wait_recv()
        first, row = ((RISE_X, 1), (FALL_X, 21))[way]
        for f in range(9):
            place = first + f if f < 5 else MASS + f - 5
            for h in range(2):
                EP[h, place, pl.ds(row, 2), :] = XR[way, f * 2 + h]
                if place == 0:
                    EP[h, 16, pl.ds(row, 2), :] = XR[way, f * 2 + h]
    for way, (first, zi) in enumerate(((RISE_Z, 2), (FALL_Z, 1))):
        for f in range(9):
            place = first + f if f < 5 else MASS + f - 5
            for h in range(2):
                ZS[way, h * 9 + f, pl.ds(0, 6), :] = EP[h, place, pl.ds(zi, 6, stride=4), :]
    face_z = [
        remote(ZS.at[0, :, pl.ds(0, 6)], ZR.at[0, :, pl.ds(0, 6)], pz_s.at[0], pz_r.at[0], UPY),
        remote(ZS.at[1, :, pl.ds(0, 6)], ZR.at[1, :, pl.ds(0, 6)], pz_s.at[1], pz_r.at[1], DNY),
    ]
    for copy in face_z:
        copy.start()

    own = pl.ds(pl.multiple_of(gy * 8, 8), 8)
    RM[own, :] = SM[own, :]

    @pl.loop(1, n)
    def _(k):
        frm = lax.rem(gy + k, n)
        moment_copy(frm, frm, frm).wait_recv()

    both = jnp.concatenate([RM[pl.ds(zl, n, stride=8), :] for zl in range(2)], axis=0)
    shape = (2 * n, L)
    row = iota(shape, 0)
    pick = iota(shape, 1) // 2 == 2 * lax.rem(row, n) + row // n
    wide = t_dot(both, jnp.where(pick, 1.0, 0.0).astype(F32))
    for y in range(8):
        MQ[pl.ds(y * 32, 16), :] = wide[y * 16:(y + 1) * 16]
        MQ[pl.ds(y * 32 + 16, 16), :] = wide[y * 16:(y + 1) * 16]

    for copy in halo_y + corners:
        copy.wait_recv()

    def turn(value, by):
        return pltpu.roll(value, by % L, 1)

    def lap(ref, i, r0, rows):
        c = ref[i, pl.ds(r0, rows), :]
        return c, (
            -6.0 * c + ref[i - 1, pl.ds(r0, rows), :] + ref[i + 1, pl.ds(r0, rows), :]
            + ref[i, pl.ds(r0 - 1, rows), :] + ref[i, pl.ds(r0 + 1, rows), :]
            + turn(c, 1) + turn(c, -1)
        )

    def potential(src, layers):
        @pl.loop(0, layers + 2)
        def _(i):
            L1[i, pl.ds(0, 24), :] = lap(src, i + 1, 6, 24)[1]

        @pl.loop(0, layers)
        def _(j):
            c, second = lap(L1, j + 1, 1, 24)
            rho = src[j + 2, pl.ds(7, 24), :]
            PT[j, pl.ds(0, 24), :] = (
                (QUENCH + 1.0) * rho + 2.0 * c + second + rho * rho * rho
            )

    potential(E, 14)

    scale = -0.5 * FORCE_UNIT * 0.125
    zeros = jnp.zeros((16, L), F32)
    for extra in range(8, 16):
        FB[pl.ds(extra, 16, stride=16), :] = zeros
    for xi in range(6):
        sums = [None, None, None]
        for k in (2 * xi, 2 * xi + 1):
            rho = E[k + 3, pl.ds(8, 16), :] * scale
            mid = PT[k + 1, pl.ds(1, 16), :]
            parts = (
                PT[k + 2, pl.ds(1, 16), :] - PT[k, pl.ds(1, 16), :],
                PT[k + 1, pl.ds(2, 16), :] - PT[k + 1, pl.ds(0, 16), :],
                turn(mid, -1) - turn(mid, 1),
            )
            for c in range(3):
                value = rho * parts[c]
                sums[c] = value if sums[c] is None else sums[c] + value
        for c in range(3):
            cx = c * 6 + xi
            if 1 <= xi <= 4:
                SP[c * 4 + xi - 1] = sums[c]
            if cx < 16:
                FA[pl.ds(cx, 16, stride=16), :] = sums[c]
            else:
                for zl in range(4):
                    FB[pl.ds((cx - 16) * 4 + zl, 16, stride=16), :] = turn(
                        sums[c], -2 * (zl - 1)
                    )
    shape = (4 * n, L)
    row = iota(shape, 0)
    window = lax.rem(2 * lax.rem(row, n) - 1 + row // n + 2 * n, 2 * n)
    choose = jnp.where(iota(shape, 1) // 2 == window, 1.0, 0.0).astype(F32)
    ga = jnp.concatenate(
        [FA[pl.ds(32 * y, 16), :] + FA[pl.ds(32 * y + 16, 16), :] for y in range(8)], axis=0
    )
    gb = jnp.concatenate(
        [FB[pl.ds(32 * y, 16), :] + FB[pl.ds(32 * y + 16, 16), :] for y in range(8)], axis=0
    )
    ta = dot_t(choose, ga)
    tb = dot_t(choose[n:2 * n], gb)
    for zl in range(4):
        SF[pl.ds(zl, n, stride=8), :] = ta[zl * n:(zl + 1) * n]
    SF[pl.ds(4, n, stride=8), :] = tb

    @pl.loop(1, n)
    def _(k):
        to = lax.rem(gy + k, n)
        force_copy(to, to, gy).start()

    for slot in range(5):
        RF[pl.ds(gy * 8 + slot, 1), :] = SF[pl.ds(gy * 8 + slot, 1), :]

    even_y = lax.rem(iota((16, L), 0), 2) == 0
    even_z = lax.rem(iota((16, L), 1), 2) == 0

    def fine_speed(x):
        mass = MQ[pl.ds(x, 16, stride=16), :]
        inverse = SPEED_UNIT * 0.5 / mass
        out = []
        for c in range(3):
            s = SP[c * 4 + x]
            s = s + jnp.where(even_y, pltpu.roll(s, 15, 0), pltpu.roll(s, 1, 0))
            s = s + jnp.where(even_z, turn(s, -1), turn(s, 1))
            m = MQ[pl.ds((c + 1) * 4 + x, 16, stride=16), :]
            out.append((m + 0.5 * s) * inverse)
        return out

    def advance(src, e, p, speed):
        mid = src[e, pl.ds(8, 16), :]
        advect = (
            speed[0] * (src[e + 1, pl.ds(8, 16), :] - src[e - 1, pl.ds(8, 16), :])
            + speed[1] * (src[e, pl.ds(9, 16), :] - src[e, pl.ds(7, 16), :])
            + speed[2] * (turn(mid, -1) - turn(mid, 1))
        )
        return mid + TIME_STEP * (lap(PT, p, 1, 16)[1] - advect)

    for x in range(4):
        speed = fine_speed(x)
        for c in range(3):
            SP[c * 4 + x] = speed[c]
        for k in (2 * x, 2 * x + 1):
            E1[k + 3, pl.ds(8, 16), :] = advance(E, k + 5, k + 3, speed)

    again_x = x_pair(E1, 3, 3, x2_s, x2_r)
    again_y = y_pair(E1, 3, 8, y2_s, y2_r, 0)
    for copy in again_x + again_y:
        copy.start()

    for way in range(2):
        face_z[way].wait_recv()
        first, zi = ((RISE_Z, 0), (FALL_Z, 3))[way]
        for f in range(9):
            place = first + f if f < 5 else MASS + f - 5
            if place == 16:
                place = 0
            for h in range(2):
                EP[h, place, pl.ds(zi, 6, stride=4), :] = ZR[way, h * 9 + f, pl.ds(0, 6), :]

    corners2 = []
    for way in range(2):
        again_x[way].wait_recv()
        for copy in y_pair(E1, 1 if way == 0 else 11, 2, c2_s, c2_r, 2 * way):
            copy.start()
            corners2.append(copy)

    @pl.loop(1, n)
    def _(k):
        frm = lax.rem(gy + k, n)
        force_copy(frm, frm, frm).wait_recv()

    half = n // 2
    expand = jnp.where(iota((half, L), 1) // 8 == iota((half, L), 0), 1.0, 0.0).astype(F32)
    for slot in range(5):
        whole = RF[pl.ds(slot, n, stride=8), :]
        for h in range(2):
            q = t_dot(whole[h * half:(h + 1) * half], expand)
            value = q[0:16]
            for y in range(1, 8):
                value = jnp.where(lax.rem(lane, 8) == y, q[y * 16:(y + 1) * 16], value)
            if slot < 4:
                FR[h, pl.ds(slot, 16, stride=4), :] = value
            else:
                FR[h, pl.ds(64, 16), :] = value

    state = []
    for h in range(2):
        mass = EP[h, MASS]
        inverse = 1.0 / mass
        force = [FR[h, pl.ds(c * 24, 24), :] for c in range(3)]
        flow = [(EP[h, MASS + 1 + c] + 0.5 * force[c]) * inverse for c in range(3)]
        square = flow[0] * flow[0] + flow[1] * flow[1] + flow[2] * flow[2]
        work = flow[0] * force[0] + flow[1] * force[1] + flow[2] * force[2]
        state.append((mass, force, flow, 1.0 - 1.5 * square, work))
    rate = 1.0 / RELAX_TIME
    gain = 1.0 - 0.5 / RELAX_TIME

    def along(speed, vector):
        out = None
        for c in range(3):
            if speed[c] == 1:
                out = vector[c] if out is None else out + vector[c]
            elif speed[c] == -1:
                out = -vector[c] if out is None else out - vector[c]
        return out

    for member in range(19):
        cx, cy, cz = SPEEDS[member]
        w = WEIGHTS[member]
        parts = []
        for h in range(2):
            mass, force, flow, rest, work = state[h]
            p = EP[h, SLOT[member]]
            if member == 0:
                new = (rate * w) * mass * rest - (3.0 * gain * w) * work
            else:
                cu, cf = along(SPEEDS[member], flow), along(SPEEDS[member], force)
                new = (rate * w) * mass * (rest + cu * (3.0 + 4.5 * cu)) + (gain * w) * (
                    3.0 * (cf - work) + 9.0 * cu * cf
                )
            parts.append(p * (1.0 - rate) + new)
        if cy:
            turned = [pltpu.roll(v, cy % L, 1) for v in parts]
            edge = lane == (0 if cy == 1 else L - 1)
            parts = [jnp.where(edge, turned[1 - h], turned[h]) for h in range(2)]
        for h in range(2):
            RS[member, h] = parts[h]
            for x in range(4):
                OP[member, x, :, pl.ds(h * L, L)] = RS[
                    member, h, pl.ds((x + 1 - cx) * 4 + 1 - cz, 2), :
                ]
    pops_end = pltpu.make_async_copy(OP, pops_out, opsem)
    pops_end.start()

    for copy in again_y + corners2:
        copy.wait_recv()
    potential(E1, 10)
    for x in range(4):
        speed = [SP[c * 4 + x] for c in range(3)]
        for k in (2 * x, 2 * x + 1):
            OD[k] = advance(E1, k + 3, k + 1, speed)
    dens_end = pltpu.make_async_copy(OD, dens_out, odsem)
    dens_end.start()

    for copy in halo_x + halo_y + corners + face_x + face_z + again_x + again_y + corners2:
        copy.wait_send()

    @pl.loop(1, n)
    def _(k):
        to = lax.rem(gy + k, n)
        moment_copy(to, to, gy).wait_send()
        force_copy(to, to, gy).wait_send()

    pops_end.wait()
    dens_end.wait()


def solution(mesh):
    nx, n = mesh.shape["gx"], mesh.shape["gy"]
    L = 4 * n

    def local(density, populations):
        vmem = lambda *shape: pltpu.VMEM(shape, F32)
        dma = lambda *shape: pltpu.SemaphoreType.DMA(shape)
        any_spec = pl.BlockSpec(memory_space=pl.ANY)
        return pl.pallas_call(
            lambda *refs: kernel(nx, n, *refs),
            out_shape=(
                jax.ShapeDtypeStruct((8, 16, L), F32),
                jax.ShapeDtypeStruct((19, 4, 2, 2 * L), F32),
            ),
            in_specs=[any_spec, any_spec],
            out_specs=(any_spec, any_spec),
            scratch_shapes=[
                vmem(18, 32, L), vmem(14, 32, L), vmem(16, 32, L), vmem(14, 32, L),
                vmem(256, L), vmem(256, L), vmem(12, 16, L),
                vmem(n * 8, 128), vmem(n * 8, 128), vmem(n * 8, 128), vmem(n * 8, 128),
                vmem(256, L), vmem(2, 16, L), vmem(19, 4, 2, 2 * L),
                vmem(2, FIELDS, 24, L), vmem(2, 18, 2, L), vmem(2, 18, 2, L),
                vmem(2, 18, 8, L), vmem(2, 18, 8, L), vmem(2, 80, L),
                vmem(19, 2, 24, L), vmem(19, 4, 2, 2 * L), vmem(8, 16, L),
                pltpu.SemaphoreType.DMA, pltpu.SemaphoreType.DMA,
                pltpu.SemaphoreType.DMA, pltpu.SemaphoreType.DMA,
                dma(2), dma(2), dma(2), dma(2), dma(4), dma(4),
                dma(2), dma(2), dma(2), dma(2), dma(4), dma(4),
                dma(2), dma(2), dma(2), dma(2),
                dma(n), dma(n), dma(n), dma(n),
            ],
            compiler_params=pltpu.CompilerParams(collective_id=0, has_side_effects=True),
        )(density, populations)

    return jax.shard_map(
        local,
        mesh=mesh,
        in_specs=(P("gx", "gy", None), P(None, "gx", "gy", None)),
        out_specs=(P("gx", "gy", None), P(None, "gx", "gy", None)),
        check_vma=False,
    )
```

time: 169 us -> 47.3 us (0.28)
  the two profiles are of different devices: /device:TPU:103 before, /device:TPU:1 now
where the time goes in v1:
time: 47.3 us; the launch traced here: 47.1 us
  Pallas kernels  43.4 us (92%)
  local copies, waits for them, and re-layouts  3.06 us (6%)
  between operations  0.64 us (1%)
    pallas_call x1, Pallas kernels, local(): pl.pallas_call(lambda *refs: kernel(nx, n, *refs), out_shape=(jax.ShapeDt...  43.4 us
    unnamed x2, local copies, waits for them, and re-layouts  3.06 us

profile of v1, /device:TPU:1, one launch (start us, length us, event | category | flops | bytes accessed | tf_op | source)
XLA Modules:
  0.0 47.1 jit_solution(517768698307986982)
XLA Ops:
  0.6 43.4 %shard_map.41 = (f32[8,16,128]{2,1,0:T(8,128)}, f32[19,4,2,256]{3,2,1,0:T(2,128)}) custom-call(f32[8,16,128]{2,1,0:T(8,128)} %refs_0_.1, f32[19,4,2,256]{3,2,1,0:T(2,128)} %refs_1_.1), custom_call_target="tpu_custom_call" | custom-call | tf_op jit(solution)/shard_map/pallas_call | solution.py:460
  44.1 1.5 %copy.6 = f32[8,16,128]{2,1,0:T(8,128)} copy(f32[8,16,128]{2,1,0:T(8,128)} %get-tuple-element.4) | data formatting | bytes 131072
  45.5 1.6 %copy.7 = f32[19,4,2,256]{3,2,1,0:T(2,128)} copy(f32[19,4,2,256]{3,2,1,0:T(2,128)} %get-tuple-element.5) | data formatting | bytes 311296

commit v2 on v1

v2 whole, which is shorter than its diff:
```python
import jax
import jax.numpy as jnp
from jax import lax
from jax.experimental import pallas as pl
from jax.experimental.pallas import tpu as pltpu
from jax.sharding import PartitionSpec as P

MESH = pl.DeviceIdType.MESH
EXACT = lax.Precision.HIGHEST
F32 = jnp.float32

TIME_STEP = 0.0008
FORCE_UNIT = 0.005
SPEED_UNIT = 2000.0
RELAX_TIME = 0.8
QUENCH = -0.25

SPEEDS = [
    (0, 0, 0),
    (1, 0, 0), (-1, 0, 0), (0, 1, 0), (0, -1, 0), (0, 0, 1), (0, 0, -1),
    (1, 1, 0), (-1, -1, 0), (1, -1, 0), (-1, 1, 0),
    (1, 0, 1), (-1, 0, -1), (1, 0, -1), (-1, 0, 1),
    (0, 1, 1), (0, -1, -1), (0, 1, -1), (0, -1, 1),
]
WEIGHTS = [1.0 / 3.0] + [1.0 / 18.0] * 6 + [1.0 / 36.0] * 12

MASS = 19
FIELDS = 23
RISE_X = [q for q in range(19) if SPEEDS[q][0] == 1]
FALL_X = [q for q in range(19) if SPEEDS[q][0] == -1]
RISE_Z = [q for q in range(19) if SPEEDS[q][2] == 1]
FALL_Z = [q for q in range(19) if SPEEDS[q][2] == -1]
MOMENTS = [MASS, MASS + 1, MASS + 2, MASS + 3]
DIAGONALS = [(1, 1), (1, -1), (-1, 1), (-1, -1)]


def dot_t(a, b):
    return lax.dot_general(
        a, b, (((1,), (1,)), ((), ())), precision=EXACT, preferred_element_type=F32
    )


def t_dot(a, b):
    return lax.dot_general(
        a, b, (((0,), (0,)), ((), ())), precision=EXACT, preferred_element_type=F32
    )


def iota(shape, dim):
    return lax.broadcasted_iota(jnp.int32, shape, dim)


def kernel(
    nx, n, dens_hbm, pops_hbm, OD, OP,
    E, E1, L1, PT, FA, FB, SP, SF, RF, SM, RM, MQ, MX, PV, EP, XS, XR, ZS, ZR, DS, DR, FR, RS,
    dsem, psem, dx_s, dx_r, dy_s, dy_r, dd_s, dd_r, px_s, px_r, pz_s, pz_r, pd_s, pd_r,
    ms_s, ms_r, fs_s, fs_r,
):
    L = 4 * n
    gx = lax.axis_index("gx")
    gy = lax.axis_index("gy")

    def place(sx, sy):
        return {"gx": lax.rem(gx + sx + nx, nx), "gy": lax.rem(gy + sy + n, n)}

    barrier = pltpu.get_barrier_semaphore()
    for sx, sy in DIAGONALS + [(1, 0), (-1, 0)]:
        pl.semaphore_signal(barrier, inc=1, device_id=place(sx, sy), device_id_type=MESH)

    @pl.loop(1, n)
    def _(k):
        pl.semaphore_signal(barrier, inc=1, device_id=place(0, k), device_id_type=MESH)

    dens_in = pltpu.make_async_copy(dens_hbm, E.at[pl.ds(7, 8), pl.ds(8, 16)], dsem)
    dens_in.start()
    pops_in = pltpu.make_async_copy(pops_hbm, PV, psem)
    pops_in.start()

    def remote(src, dst, send, recv, where):
        return pltpu.make_async_remote_copy(
            src_ref=src, dst_ref=dst, send_sem=send, recv_sem=recv, device_id=where,
            device_id_type=MESH,
        )

    def block(x0, xs, y0, ys):
        return E.at[pl.ds(x0, xs), pl.ds(y0, ys)]

    dens_in.wait()
    pl.semaphore_wait(barrier, n + 5)

    halo = []
    for i, (sx, sy) in enumerate(DIAGONALS):
        x0, x1 = (9, 1) if sx == 1 else (7, 15)
        y0, y1 = (18, 2) if sy == 1 else (8, 24)
        halo.append(remote(
            block(x0, 6, y0, 6), block(x1, 6, y1, 6), dd_s.at[i], dd_r.at[i], place(sx, sy)
        ))
    halo += [
        remote(block(8, 7, 8, 16), block(0, 7, 8, 16), dx_s.at[0], dx_r.at[0], place(1, 0)),
        remote(block(7, 7, 8, 16), block(15, 7, 8, 16), dx_s.at[1], dx_r.at[1], place(-1, 0)),
        remote(block(7, 8, 17, 7), block(7, 8, 1, 7), dy_s.at[0], dy_r.at[0], place(0, 1)),
        remote(block(7, 8, 8, 7), block(7, 8, 24, 7), dy_s.at[1], dy_r.at[1], place(0, -1)),
    ]
    for copy in halo:
        copy.start()

    lane = iota((1, L), 1)

    pops_in.wait()
    for h in range(2):
        for member in range(19):
            for x in range(4):
                EP[h, member, pl.ds(x * 4 + 5, 2), :] = PV[member, x, :, pl.ds(h * L, L)]
        total = jnp.zeros((24, L), F32)
        moment = [jnp.zeros((24, L), F32) for _ in range(3)]
        for member in range(19):
            value = EP[h, member]
            total = total + value
            for c in range(3):
                if SPEEDS[member][c] == 1:
                    moment[c] = moment[c] + value
                elif SPEEDS[member][c] == -1:
                    moment[c] = moment[c] - value
        EP[h, MASS] = total
        for c in range(3):
            EP[h, MASS + 1 + c] = moment[c]

    for way, (members, row, rows) in enumerate(
        ((RISE_X, 17, (13, 17)), (FALL_X, 5, (5, 9)))
    ):
        for h in range(2):
            for f in range(5):
                XS[way, f * 2 + h] = EP[h, members[f], pl.ds(row, 2), :]
            for c in range(4):
                for layer in range(2):
                    XS[way, 10 + (c * 2 + layer) * 2 + h] = EP[
                        h, MASS + c, pl.ds(rows[layer], 2), :
                    ]
    face_x = [
        remote(XS.at[0], XR.at[0], px_s.at[0], px_r.at[0], place(1, 0)),
        remote(XS.at[1], XR.at[1], px_s.at[1], px_r.at[1], place(-1, 0)),
    ]
    for copy in face_x:
        copy.start()

    for way, (members, zi) in enumerate(((RISE_Z, 2), (FALL_Z, 1))):
        for f, field in enumerate(members + MOMENTS):
            for h in range(2):
                ZS[way, f * 2 + h] = EP[h, field, pl.ds(4 + zi, 4, stride=4), :]
    for i, (sx, sy) in enumerate(DIAGONALS):
        row = (16 if sx == 1 else 4) + (2 if sy == 1 else 1)
        for f, field in enumerate([SPEEDS.index((sx, 0, sy))] + MOMENTS):
            for h in range(2):
                DS[i, pl.ds(f * 2 + h, 1), :] = EP[h, field, pl.ds(row, 1), :]
    face_z = [
        remote(ZS.at[0], ZR.at[0], pz_s.at[0], pz_r.at[0], place(0, 1)),
        remote(ZS.at[1], ZR.at[1], pz_s.at[1], pz_r.at[1], place(0, -1)),
    ]
    edges = [
        remote(DS.at[i], DR.at[i], pd_s.at[i], pd_r.at[i], place(sx, sy))
        for i, (sx, sy) in enumerate(DIAGONALS)
    ]
    for copy in edges + face_z:
        copy.start()

    for h in range(2):
        for zl in range(2):
            for c in range(4):
                MX[zl, h, pl.ds(c * 8 + 2, 4), :] = EP[h, MASS + c, pl.ds(5 + zl, 4, stride=4), :]
    for way in range(2):
        face_x[way].wait_recv()
        for h in range(2):
            for c in range(4):
                for layer in range(2):
                    both = XR[way, 10 + (c * 2 + layer) * 2 + h]
                    for zl in range(2):
                        MX[zl, h, pl.ds(c * 8 + way * 6 + layer, 1), :] = both[zl:zl + 1]
    shape = (3 * n, L)
    row, col = iota(shape, 0), iota(shape, 1)
    spread = []
    for h in range(2):
        t = lax.rem(col + (h * L + 2 + 8 * n) - 4 * (row // n), 8 * n)
        hit = jnp.logical_and(t // 8 == lax.rem(row, n), lax.rem(t, 8) < 4)
        spread.append(jnp.where(hit, 1.0, 0.0).astype(F32))
    for zl in range(2):
        result = None
        for h in range(2):
            values = MX[zl, h]
            tiles = jnp.concatenate(
                [jnp.where(lax.rem(lane + 2, 4) == y, values, 0.0) for y in range(4)], axis=0
            )
            part = dot_t(spread[h], tiles)
            result = part if result is None else result + part
        for yg in range(3):
            SM[pl.ds(zl * 3 + yg, n, stride=8), :] = result[yg * n:(yg + 1) * n]

    def moment_copy(to, sem_to, slot):
        return remote(
            SM.at[pl.ds(pl.multiple_of(to * 8, 8), 6)],
            RM.at[pl.ds(pl.multiple_of(slot * 8, 8), 6)],
            ms_s.at[sem_to], ms_r.at[slot], {"gx": gx, "gy": to},
        )

    def force_copy(to, sem_to, slot):
        return remote(
            SF.at[pl.ds(pl.multiple_of(to * 8, 8), 5)],
            RF.at[pl.ds(pl.multiple_of(slot * 8, 8), 5)],
            fs_s.at[sem_to], fs_r.at[slot], {"gx": gx, "gy": to},
        )

    @pl.loop(1, n)
    def _(k):
        to = lax.rem(gy + k, n)
        moment_copy(to, to, gy).start()

    for slot in range(6):
        RM[pl.ds(gy * 8 + slot, 1), :] = SM[pl.ds(gy * 8 + slot, 1), :]

    for way, (members, row, layer) in enumerate(((RISE_X, 1, 1), (FALL_X, 21, 0))):
        for h in range(2):
            for f in range(5):
                EP[h, members[f], pl.ds(row, 2), :] = XR[way, f * 2 + h]
            for c in range(4):
                EP[h, MASS + c, pl.ds(row, 2), :] = XR[way, 10 + (c * 2 + layer) * 2 + h]

    def turn(value, by):
        return pltpu.roll(value, by % L, 1)

    def lap(ref, i, r0, rows):
        c = ref[i, pl.ds(r0, rows), :]
        return c, (
            -6.0 * c + ref[i - 1, pl.ds(r0, rows), :] + ref[i + 1, pl.ds(r0, rows), :]
            + ref[i, pl.ds(r0 - 1, rows), :] + ref[i, pl.ds(r0 + 1, rows), :]
            + turn(c, 1) + turn(c, -1)
        )

    def potential(src, layers, r0, rows):
        @pl.loop(0, layers + 2)
        def _(i):
            L1[i, pl.ds(0, rows), :] = lap(src, i + 1, r0, rows)[1]

        @pl.loop(0, layers)
        def _(j):
            c, second = lap(L1, j + 1, 1, rows)
            rho = src[j + 2, pl.ds(r0 + 1, rows), :]
            PT[j, pl.ds(0, rows), :] = (
                (QUENCH + 1.0) * rho + 2.0 * c + second + rho * rho * rho
            )

    for copy in halo:
        copy.wait_recv()
    potential(E, 18, 2, 32)

    scale = -0.5 * FORCE_UNIT * 0.125
    zeros = jnp.zeros((16, L), F32)
    for extra in range(8, 16):
        FB[pl.ds(extra, 16, stride=16), :] = zeros

    def force_pair(x8):
        sums = [None, None, None]
        for k in (2 * x8, 2 * x8 + 1):
            rho = E[k + 3, pl.ds(4, 24), :] * scale
            mid = PT[k + 1, pl.ds(1, 24), :]
            parts = (
                PT[k + 2, pl.ds(1, 24), :] - PT[k, pl.ds(1, 24), :],
                PT[k + 1, pl.ds(2, 24), :] - PT[k + 1, pl.ds(0, 24), :],
                turn(mid, -1) - turn(mid, 1),
            )
            for c in range(3):
                value = rho * parts[c]
                sums[c] = value if sums[c] is None else sums[c] + value
        for c in range(3):
            SP[c * 8 + x8] = sums[c]

    for x8 in range(1, 7):
        force_pair(x8)
        for c in range(3):
            cx = c * 6 + x8 - 1
            own = SP[c * 8 + x8, pl.ds(4, 16), :]
            if cx < 16:
                FA[pl.ds(cx, 16, stride=16), :] = own
            else:
                for zl in range(4):
                    FB[pl.ds((cx - 16) * 4 + zl, 16, stride=16), :] = turn(own, -2 * (zl - 1))
    shape = (4 * n, L)
    row = iota(shape, 0)
    window = lax.rem(2 * lax.rem(row, n) - 1 + row // n + 2 * n, 2 * n)
    choose = jnp.where(iota(shape, 1) // 2 == window, 1.0, 0.0).astype(F32)
    ga = jnp.concatenate(
        [FA[pl.ds(32 * y, 16), :] + FA[pl.ds(32 * y + 16, 16), :] for y in range(8)], axis=0
    )
    gb = jnp.concatenate(
        [FB[pl.ds(32 * y, 16), :] + FB[pl.ds(32 * y + 16, 16), :] for y in range(8)], axis=0
    )
    ta = dot_t(choose, ga)
    tb = dot_t(choose[n:2 * n], gb)
    for zl in range(4):
        SF[pl.ds(zl, n, stride=8), :] = ta[zl * n:(zl + 1) * n]
    SF[pl.ds(4, n, stride=8), :] = tb

    @pl.loop(1, n)
    def _(k):
        to = lax.rem(gy + k, n)
        force_copy(to, to, gy).start()

    for slot in range(5):
        RF[pl.ds(gy * 8 + slot, 1), :] = SF[pl.ds(gy * 8 + slot, 1), :]
    force_pair(0)
    force_pair(7)

    for way, (members, zi) in enumerate(((RISE_Z, 0), (FALL_Z, 3))):
        face_z[way].wait_recv()
        for f, field in enumerate(members + MOMENTS):
            for h in range(2):
                EP[h, field, pl.ds(4 + zi, 4, stride=4), :] = ZR[way, f * 2 + h]
    for i, (sx, sy) in enumerate(DIAGONALS):
        edges[i].wait_recv()
        row = (0 if sx == 1 else 20) + (0 if sy == 1 else 3)
        for f, field in enumerate([SPEEDS.index((sx, 0, sy))] + MOMENTS):
            for h in range(2):
                EP[h, field, pl.ds(row, 1), :] = DR[i, pl.ds(f * 2 + h, 1), :]

    @pl.loop(1, n)
    def _(k):
        frm = lax.rem(gy + k, n)
        moment_copy(frm, frm, frm).wait_recv()

    shape = (2 * n, L)
    row = iota(shape, 0)
    pick = iota(shape, 1) // 2 == 2 * lax.rem(row, n) + row // n
    pick = jnp.where(pick, 1.0, 0.0).astype(F32)
    for yg in range(3):
        both = jnp.concatenate(
            [RM[pl.ds(zl * 3 + yg, n, stride=8), :] for zl in range(2)], axis=0
        )
        wide = t_dot(both, pick)
        for y in range(4):
            for k in range(2):
                MQ[pl.ds(((yg * 4 + y) * 2 + k) * 32, 32), :] = wide[y * 32:(y + 1) * 32]

    even_y = lax.rem(iota((24, L), 0), 2) == 0
    even_z = lax.rem(iota((24, L), 1), 2) == 0

    def fine_speed(x8):
        mass = MQ[pl.ds(x8, 24, stride=32), :]
        inverse = SPEED_UNIT * 0.5 / mass
        out = []
        for c in range(3):
            s = SP[c * 8 + x8]
            s = s + jnp.where(even_y, pltpu.roll(s, 23, 0), pltpu.roll(s, 1, 0))
            s = s + jnp.where(even_z, turn(s, -1), turn(s, 1))
            m = MQ[pl.ds((c + 1) * 8 + x8, 24, stride=32), :]
            out.append((m + 0.5 * s) * inverse)
        return out

    def advance(src, e, r0, p, rows, speed):
        mid = src[e, pl.ds(r0, rows), :]
        advect = (
            speed[0] * (src[e + 1, pl.ds(r0, rows), :] - src[e - 1, pl.ds(r0, rows), :])
            + speed[1] * (src[e, pl.ds(r0 + 1, rows), :] - src[e, pl.ds(r0 - 1, rows), :])
            + speed[2] * (turn(mid, -1) - turn(mid, 1))
        )
        return mid + TIME_STEP * (lap(PT, p, 1, rows)[1] - advect)

    for x8 in range(8):
        speed = fine_speed(x8)
        if 2 <= x8 <= 5:
            for c in range(3):
                SP[c * 8 + x8] = speed[c]
        for d in (2 * x8 - 1, 2 * x8):
            if 0 <= d < 14:
                E1[d, pl.ds(4, 24), :] = advance(E, d + 4, 4, d + 2, 24, speed)

    potential(E1, 10, 6, 24)
    for x in range(4):
        speed = [SP[c * 8 + x + 2, pl.ds(4, 16), :] for c in range(3)]
        for k in (2 * x, 2 * x + 1):
            OD[k] = advance(E1, k + 3, 8, k + 1, 16, speed)

    @pl.loop(1, n)
    def _(k):
        frm = lax.rem(gy + k, n)
        force_copy(frm, frm, frm).wait_recv()

    half = n // 2
    expand = jnp.where(iota((half, L), 1) // 8 == iota((half, L), 0), 1.0, 0.0).astype(F32)
    for slot in range(5):
        whole = RF[pl.ds(slot, n, stride=8), :]
        for h in range(2):
            q = t_dot(whole[h * half:(h + 1) * half], expand)
            value = q[0:16]
            for y in range(1, 8):
                value = jnp.where(lax.rem(lane, 8) == y, q[y * 16:(y + 1) * 16], value)
            if slot < 4:
                FR[h, pl.ds(slot, 16, stride=4), :] = value
            else:
                FR[h, pl.ds(64, 16), :] = value

    state = []
    for h in range(2):
        mass = EP[h, MASS]
        inverse = 1.0 / mass
        force = [FR[h, pl.ds(c * 24, 24), :] for c in range(3)]
        flow = [(EP[h, MASS + 1 + c] + 0.5 * force[c]) * inverse for c in range(3)]
        square = flow[0] * flow[0] + flow[1] * flow[1] + flow[2] * flow[2]
        work = flow[0] * force[0] + flow[1] * force[1] + flow[2] * force[2]
        state.append((mass, force, flow, 1.0 - 1.5 * square, work))
    rate = 1.0 / RELAX_TIME
    gain = 1.0 - 0.5 / RELAX_TIME

    def along(speed, vector):
        out = None
        for c in range(3):
            if speed[c] == 1:
                out = vector[c] if out is None else out + vector[c]
            elif speed[c] == -1:
                out = -vector[c] if out is None else out - vector[c]
        return out

    for member in range(19):
        cx, cy, cz = SPEEDS[member]
        w = WEIGHTS[member]
        parts = []
        for h in range(2):
            mass, force, flow, rest, work = state[h]
            p = EP[h, member]
            if member == 0:
                new = (rate * w) * mass * rest - (3.0 * gain * w) * work
            else:
                cu, cf = along(SPEEDS[member], flow), along(SPEEDS[member], force)
                new = (rate * w) * mass * (rest + cu * (3.0 + 4.5 * cu)) + (gain * w) * (
                    3.0 * (cf - work) + 9.0 * cu * cf
                )
            parts.append(p * (1.0 - rate) + new)
        if cy:
            turned = [pltpu.roll(v, cy % L, 1) for v in parts]
            edge = lane == (0 if cy == 1 else L - 1)
            parts = [jnp.where(edge, turned[1 - h], turned[h]) for h in range(2)]
        for h in range(2):
            RS[member, h] = parts[h]
            for x in range(4):
                OP[member, x, :, pl.ds(h * L, L)] = RS[
                    member, h, pl.ds((x + 1 - cx) * 4 + 1 - cz, 2), :
                ]

    for copy in halo + face_x + face_z + edges:
        copy.wait_send()

    @pl.loop(1, n)
    def _(k):
        to = lax.rem(gy + k, n)
        moment_copy(to, to, gy).wait_send()
        force_copy(to, to, gy).wait_send()


def put(dens, pops, dens_out, pops_out, dsem, psem):
    first = pltpu.make_async_copy(dens, dens_out, dsem)
    second = pltpu.make_async_copy(pops, pops_out, psem)
    second.start()
    first.start()
    first.wait()
    second.wait()


def solution(mesh):
    nx, n = mesh.shape["gx"], mesh.shape["gy"]
    L = 4 * n

    def local(density, populations):
        vmem = lambda *shape: pltpu.VMEM(shape, F32)
        dma = lambda *shape: pltpu.SemaphoreType.DMA(shape)
        any_spec = pl.BlockSpec(memory_space=pl.ANY)
        vmem_spec = pl.BlockSpec(memory_space=pltpu.VMEM)
        shapes = (
            jax.ShapeDtypeStruct((8, 16, L), F32),
            jax.ShapeDtypeStruct((19, 4, 2, 2 * L), F32),
        )
        density = pltpu.with_memory_space_constraint(density, pltpu.HBM)
        populations = pltpu.with_memory_space_constraint(populations, pltpu.HBM)
        density, populations = pl.pallas_call(
            lambda *refs: kernel(nx, n, *refs),
            out_shape=shapes,
            in_specs=[any_spec, any_spec],
            out_specs=(vmem_spec, vmem_spec),
            scratch_shapes=[
                vmem(22, 40, L), vmem(14, 32, L), vmem(20, 40, L), vmem(18, 32, L),
                vmem(256, L), vmem(256, L), vmem(24, 24, L),
                vmem(n * 8, 128), vmem(n * 8, 128), vmem(n * 8, 128), vmem(n * 8, 128),
                vmem(768, L), vmem(2, 2, 32, L), vmem(19, 4, 2, 2 * L),
                vmem(2, FIELDS, 24, L), vmem(2, 26, 2, L), vmem(2, 26, 2, L),
                vmem(2, 18, 4, L), vmem(2, 18, 4, L), vmem(4, 16, L), vmem(4, 16, L),
                vmem(2, 80, L), vmem(19, 2, 24, L),
                dma(), dma(),
                dma(2), dma(2), dma(2), dma(2), dma(4), dma(4),
                dma(2), dma(2), dma(2), dma(2), dma(4), dma(4),
                dma(n), dma(n), dma(n), dma(n),
            ],
            compiler_params=pltpu.CompilerParams(
                collective_id=0, has_side_effects=True, vmem_limit_bytes=16 * 2**20
            ),
        )(density, populations)
        return pl.pallas_call(
            put,
            out_shape=shapes,
            in_specs=[any_spec, any_spec],
            out_specs=(any_spec, any_spec),
            scratch_shapes=[dma(), dma()],
            compiler_params=pltpu.CompilerParams(vmem_limit_bytes=8 * 2**20),
        )(density, populations)

    return jax.shard_map(
        local,
        mesh=mesh,
        in_specs=(P("gx", "gy", None), P(None, "gx", "gy", None)),
        out_specs=(P("gx", "gy", None), P(None, "gx", "gy", None)),
        check_vma=False,
    )
```

time: 47.3 us -> 45.4 us (0.960)
  local copies, waits for them, and re-layouts: 3.06 us -> 0 us
  Pallas kernels: 43.4 us -> 44.7 us
    unnamed x2 -> x0, local copies, waits for them, and re-layouts: 3.06 us -> none
    pallas_call x1 -> x2, Pallas kernels: 43.4 us -> 44.7 us  [the longest x1 44 us: local(): pl.pallas_call(lambda *refs: kernel(nx, n, *refs), out_shape=shapes, in_s...]
where the time goes in v2:
time: 45.4 us; the launch traced here: 45.3 us
  Pallas kernels  44.7 us (98%)
  between operations  0.64 us (1%)
    pallas_call x1, Pallas kernels, local(): pl.pallas_call(lambda *refs: kernel(nx, n, *refs), out_shape=shapes, in_s...  44 us

profile of v2, /device:TPU:1, one launch (start us, length us, event | category | flops | bytes accessed | tf_op | source)
XLA Modules:
  0.0 45.3 jit_solution(431723894257369767)
XLA Ops:
  0.6 44.0 %shard_map.41 = (f32[8,16,128]{2,1,0:T(8,128)S(1)}, f32[19,4,2,256]{3,2,1,0:T(2,128)S(1)}) custom-call(f32[8,16,128]{2,1,0:T(8,128)} %refs_0_.1, f32[19,4,2,256]{3,2,1,0:T(2,128)} %refs_1_.1), custom_call_target="tpu_custom_call" | custom-call | tf_op jit(solution)/shard_map/pallas_call | solution.py:480
  44.6 0.7 %shard_map.42 = (f32[8,16,128]{2,1,0:T(8,128)}, f32[19,4,2,256]{3,2,1,0:T(2,128)}) custom-call(f32[8,16,128]{2,1,0:T(8,128)S(1)} %get-tuple-element.4.dens, f32[19,4,2,256]{3,2,1,0:T(2,128)S(1)} %get-tuple-element.5.pops), custom_call_target="tpu_custom_call" | custom-call | tf_op jit(solution)/shard_map/pallas_call | solution.py:502

commit v3 on v2

--- a/solution.py
+++ b/solution.py
@@ -52,8 +52,8 @@
 
 def kernel(
     nx, n, dens_hbm, pops_hbm, OD, OP,
-    E, E1, L1, PT, FA, FB, SP, SF, RF, SM, RM, MQ, MX, PV, EP, XS, XR, ZS, ZR, DS, DR, FR, RS,
-    dsem, psem, dx_s, dx_r, dy_s, dy_r, dd_s, dd_r, px_s, px_r, pz_s, pz_r, pd_s, pd_r,
+    E, E2, E1, L1, PT, FA, FB, SP, SF, RF, SM, RM, MQ, MX, PV, EP, XS, XR, ZS, ZR, DS, DR, FR, RS,
+    dsem, psem, h1_s, h1_r, h2_s, h2_r, px_s, px_r, pz_s, pz_r, pd_s, pd_r,
     ms_s, ms_r, fs_s, fs_r,
 ):
     L = 4 * n
@@ -71,7 +71,7 @@
     def _(k):
         pl.semaphore_signal(barrier, inc=1, device_id=place(0, k), device_id_type=MESH)
 
-    dens_in = pltpu.make_async_copy(dens_hbm, E.at[pl.ds(7, 8), pl.ds(8, 16)], dsem)
+    dens_in = pltpu.make_async_copy(dens_hbm, E.at[pl.ds(5, 8), pl.ds(8, 16)], dsem)
     dens_in.start()
     pops_in = pltpu.make_async_copy(pops_hbm, PV, psem)
     pops_in.start()
@@ -82,25 +82,31 @@
             device_id_type=MESH,
         )
 
-    def block(x0, xs, y0, ys):
-        return E.at[pl.ds(x0, xs), pl.ds(y0, ys)]
-
     dens_in.wait()
     pl.semaphore_wait(barrier, n + 5)
 
-    halo = []
-    for i, (sx, sy) in enumerate(DIAGONALS):
-        x0, x1 = (9, 1) if sx == 1 else (7, 15)
-        y0, y1 = (18, 2) if sy == 1 else (8, 24)
-        halo.append(remote(
-            block(x0, 6, y0, 6), block(x1, 6, y1, 6), dd_s.at[i], dd_r.at[i], place(sx, sy)
-        ))
-    halo += [
-        remote(block(8, 7, 8, 16), block(0, 7, 8, 16), dx_s.at[0], dx_r.at[0], place(1, 0)),
-        remote(block(7, 7, 8, 16), block(15, 7, 8, 16), dx_s.at[1], dx_r.at[1], place(-1, 0)),
-        remote(block(7, 8, 17, 7), block(7, 8, 1, 7), dy_s.at[0], dy_r.at[0], place(0, 1)),
-        remote(block(7, 8, 8, 7), block(7, 8, 24, 7), dy_s.at[1], dy_r.at[1], place(0, -1)),
-    ]
+    def boxes(items, target, send, recv):
+        return [
+            remote(
+                E.at[pl.ds(x0, xs), pl.ds(y0, ys)], target.at[pl.ds(x1, xs), pl.ds(y1, ys)],
+                send.at[i], recv.at[i], place(*where),
+            )
+            for i, (where, x0, x1, xs, y0, y1, ys) in enumerate(items)
+        ]
+
+    halo = boxes(
+        [
+            ((sx, sy), *((9, 1, 4) if sx == 1 else (5, 13, 4)),
+             *((21, 5, 3) if sy == 1 else (8, 24, 3)))
+            for sx, sy in DIAGONALS
+        ] + [
+            ((1, 0), 8, 0, 5, 8, 8, 16),
+            ((-1, 0), 5, 13, 5, 8, 8, 16),
+            ((0, 1), 5, 5, 8, 21, 5, 3),
+            ((0, -1), 5, 5, 8, 8, 24, 3),
+        ],
+        E, h1_s, h1_r,
+    )
     for copy in halo:
         copy.start()
 
@@ -143,24 +149,35 @@
     for copy in face_x:
         copy.start()
 
+    outer = boxes(
+        [
+            ((1, 0), 6, 0, 2, 8, 8, 16),
+            ((-1, 0), 10, 20, 2, 8, 8, 16),
+            ((0, 1), 5, 7, 8, 17, 1, 4),
+            ((0, -1), 5, 7, 8, 11, 27, 4),
+        ] + [
+            ((sx, sy), *((10, 4, 3) if sx == 1 else (5, 15, 3)),
+             *((18, 2, 3) if sy == 1 else (11, 27, 3)))
+            for sx, sy in DIAGONALS
+        ] + [
+            ((sx, sy), *((7, 1, 2) if sx == 1 else (9, 19, 2)),
+             *((22, 6, 2) if sy == 1 else (8, 24, 2)))
+            for sx, sy in DIAGONALS
+        ],
+        E2, h2_s, h2_r,
+    )
+    for copy in outer:
+        copy.start()
+
     for way, (members, zi) in enumerate(((RISE_Z, 2), (FALL_Z, 1))):
         for f, field in enumerate(members + MOMENTS):
             for h in range(2):
                 ZS[way, f * 2 + h] = EP[h, field, pl.ds(4 + zi, 4, stride=4), :]
-    for i, (sx, sy) in enumerate(DIAGONALS):
-        row = (16 if sx == 1 else 4) + (2 if sy == 1 else 1)
-        for f, field in enumerate([SPEEDS.index((sx, 0, sy))] + MOMENTS):
-            for h in range(2):
-                DS[i, pl.ds(f * 2 + h, 1), :] = EP[h, field, pl.ds(row, 1), :]
     face_z = [
         remote(ZS.at[0], ZR.at[0], pz_s.at[0], pz_r.at[0], place(0, 1)),
         remote(ZS.at[1], ZR.at[1], pz_s.at[1], pz_r.at[1], place(0, -1)),
     ]
-    edges = [
-        remote(DS.at[i], DR.at[i], pd_s.at[i], pd_r.at[i], place(sx, sy))
-        for i, (sx, sy) in enumerate(DIAGONALS)
-    ]
-    for copy in edges + face_z:
+    for copy in face_z:
         copy.start()
 
     for h in range(2):
@@ -216,6 +233,21 @@
     for slot in range(6):
         RM[pl.ds(gy * 8 + slot, 1), :] = SM[pl.ds(gy * 8 + slot, 1), :]
 
+    for way in range(2):
+        for side, (members, layer) in enumerate(((RISE_X, 1), (FALL_X, 0))):
+            member = SPEEDS.index((1 - 2 * side, 0, 1 - 2 * way))
+            picks = [members.index(member)] + [5 + c * 2 + layer for c in range(4)]
+            for f, item in enumerate(picks):
+                for h in range(2):
+                    both = XR[side, item * 2 + h]
+                    DS[way, pl.ds((side * 5 + f) * 2 + h, 1), :] = both[1 - way:2 - way]
+    edges = [
+        remote(DS.at[0], DR.at[0], pd_s.at[0], pd_r.at[0], place(0, 1)),
+        remote(DS.at[1], DR.at[1], pd_s.at[1], pd_r.at[1], place(0, -1)),
+    ]
+    for copy in edges:
+        copy.start()
+
     for way, (members, row, layer) in enumerate(((RISE_X, 1, 1), (FALL_X, 21, 0))):
         for h in range(2):
             for f in range(5):
@@ -234,54 +266,51 @@
             + turn(c, 1) + turn(c, -1)
         )
 
-    def potential(src, layers, r0, rows):
-        @pl.loop(0, layers + 2)
-        def _(i):
-            L1[i, pl.ds(0, rows), :] = lap(src, i + 1, r0, rows)[1]
-
-        @pl.loop(0, layers)
-        def _(j):
+    def potential(src, first, layers, r0, rows):
+        for i in range(layers + 2):
+            L1[i, pl.ds(0, rows), :] = lap(src, first + i + 1, r0, rows)[1]
+        for j in range(layers):
             c, second = lap(L1, j + 1, 1, rows)
-            rho = src[j + 2, pl.ds(r0 + 1, rows), :]
+            rho = src[first + j + 2, pl.ds(r0 + 1, rows), :]
             PT[j, pl.ds(0, rows), :] = (
                 (QUENCH + 1.0) * rho + 2.0 * c + second + rho * rho * rho
             )
 
     for copy in halo:
         copy.wait_recv()
-    potential(E, 18, 2, 32)
+    potential(E, 0, 14, 6, 24)
 
     scale = -0.5 * FORCE_UNIT * 0.125
     zeros = jnp.zeros((16, L), F32)
     for extra in range(8, 16):
         FB[pl.ds(extra, 16, stride=16), :] = zeros
 
-    def force_pair(x8):
+    def force_pair(src, e0, p0, r0, rows):
         sums = [None, None, None]
-        for k in (2 * x8, 2 * x8 + 1):
-            rho = E[k + 3, pl.ds(4, 24), :] * scale
-            mid = PT[k + 1, pl.ds(1, 24), :]
+        for k in range(2):
+            rho = src[e0 + k, pl.ds(r0, rows), :] * scale
+            mid = PT[p0 + k, pl.ds(1, rows), :]
             parts = (
-                PT[k + 2, pl.ds(1, 24), :] - PT[k, pl.ds(1, 24), :],
-                PT[k + 1, pl.ds(2, 24), :] - PT[k + 1, pl.ds(0, 24), :],
+                PT[p0 + k + 1, pl.ds(1, rows), :] - PT[p0 + k - 1, pl.ds(1, rows), :],
+                PT[p0 + k, pl.ds(2, rows), :] - PT[p0 + k, pl.ds(0, rows), :],
                 turn(mid, -1) - turn(mid, 1),
             )
             for c in range(3):
                 value = rho * parts[c]
                 sums[c] = value if sums[c] is None else sums[c] + value
+        return sums
+
+    for xi in range(6):
+        sums = force_pair(E, 2 * xi + 3, 2 * xi + 1, 8, 16)
         for c in range(3):
-            SP[c * 8 + x8] = sums[c]
-
-    for x8 in range(1, 7):
-        force_pair(x8)
-        for c in range(3):
-            cx = c * 6 + x8 - 1
-            own = SP[c * 8 + x8, pl.ds(4, 16), :]
+            cx = c * 6 + xi
             if cx < 16:
-                FA[pl.ds(cx, 16, stride=16), :] = own
+                FA[pl.ds(cx, 16, stride=16), :] = sums[c]
             else:
                 for zl in range(4):
-                    FB[pl.ds((cx - 16) * 4 + zl, 16, stride=16), :] = turn(own, -2 * (zl - 1))
+                    FB[pl.ds((cx - 16) * 4 + zl, 16, stride=16), :] = turn(
+                        sums[c], -2 * (zl - 1)
+                    )
     shape = (4 * n, L)
     row = iota(shape, 0)
     window = lax.rem(2 * lax.rem(row, n) - 1 + row // n + 2 * n, 2 * n)
@@ -305,20 +334,23 @@
 
     for slot in range(5):
         RF[pl.ds(gy * 8 + slot, 1), :] = SF[pl.ds(gy * 8 + slot, 1), :]
-    force_pair(0)
-    force_pair(7)
 
     for way, (members, zi) in enumerate(((RISE_Z, 0), (FALL_Z, 3))):
         face_z[way].wait_recv()
         for f, field in enumerate(members + MOMENTS):
             for h in range(2):
                 EP[h, field, pl.ds(4 + zi, 4, stride=4), :] = ZR[way, f * 2 + h]
-    for i, (sx, sy) in enumerate(DIAGONALS):
-        edges[i].wait_recv()
-        row = (0 if sx == 1 else 20) + (0 if sy == 1 else 3)
-        for f, field in enumerate([SPEEDS.index((sx, 0, sy))] + MOMENTS):
-            for h in range(2):
-                EP[h, field, pl.ds(row, 1), :] = DR[i, pl.ds(f * 2 + h, 1), :]
+
+    for copy in outer:
+        copy.wait_recv()
+    for e in range(18):
+        y0, ys = (8, 16) if e in (0, 17) else (5, 22)
+        E2[e + 2, pl.ds(y0, ys), :] = E[e, pl.ds(y0, ys), :]
+    potential(E2, 0, 18, 2, 32)
+    for x8 in range(8):
+        sums = force_pair(E2, 2 * x8 + 3, 2 * x8 + 1, 4, 24)
+        for c in range(3):
+            SP[c * 8 + x8] = sums[c]
 
     @pl.loop(1, n)
     def _(k):
@@ -369,13 +401,22 @@
                 SP[c * 8 + x8] = speed[c]
         for d in (2 * x8 - 1, 2 * x8):
             if 0 <= d < 14:
-                E1[d, pl.ds(4, 24), :] = advance(E, d + 4, 4, d + 2, 24, speed)
-
-    potential(E1, 10, 6, 24)
+                E1[d, pl.ds(4, 24), :] = advance(E2, d + 4, 4, d + 2, 24, speed)
+
+    potential(E1, 0, 10, 6, 24)
     for x in range(4):
         speed = [SP[c * 8 + x + 2, pl.ds(4, 16), :] for c in range(3)]
         for k in (2 * x, 2 * x + 1):
             OD[k] = advance(E1, k + 3, 8, k + 1, 16, speed)
+
+    for way in range(2):
+        edges[way].wait_recv()
+        for side in range(2):
+            row = side * 20 + way * 3
+            member = SPEEDS.index((1 - 2 * side, 0, 1 - 2 * way))
+            for f, field in enumerate([member] + MOMENTS):
+                for h in range(2):
+                    EP[h, field, pl.ds(row, 1), :] = DR[way, pl.ds((side * 5 + f) * 2 + h, 1), :]
 
     @pl.loop(1, n)
     def _(k):
@@ -443,7 +484,7 @@
                     member, h, pl.ds((x + 1 - cx) * 4 + 1 - cz, 2), :
                 ]
 
-    for copy in halo + face_x + face_z + edges:
+    for copy in halo + outer + face_x + face_z + edges:
         copy.wait_send()
 
     @pl.loop(1, n)
@@ -483,16 +524,17 @@
             in_specs=[any_spec, any_spec],
             out_specs=(vmem_spec, vmem_spec),
             scratch_shapes=[
-                vmem(22, 40, L), vmem(14, 32, L), vmem(20, 40, L), vmem(18, 32, L),
+                vmem(18, 32, L), vmem(22, 40, L), vmem(14, 32, L),
+                vmem(20, 40, L), vmem(18, 32, L),
                 vmem(256, L), vmem(256, L), vmem(24, 24, L),
                 vmem(n * 8, 128), vmem(n * 8, 128), vmem(n * 8, 128), vmem(n * 8, 128),
                 vmem(768, L), vmem(2, 2, 32, L), vmem(19, 4, 2, 2 * L),
                 vmem(2, FIELDS, 24, L), vmem(2, 26, 2, L), vmem(2, 26, 2, L),
-                vmem(2, 18, 4, L), vmem(2, 18, 4, L), vmem(4, 16, L), vmem(4, 16, L),
+                vmem(2, 18, 4, L), vmem(2, 18, 4, L), vmem(2, 24, L), vmem(2, 24, L),
                 vmem(2, 80, L), vmem(19, 2, 24, L),
                 dma(), dma(),
-                dma(2), dma(2), dma(2), dma(2), dma(4), dma(4),
-                dma(2), dma(2), dma(2), dma(2), dma(4), dma(4),
+                dma(8), dma(8), dma(12), dma(12),
+                dma(2), dma(2), dma(2), dma(2), dma(2), dma(2),
                 dma(n), dma(n), dma(n), dma(n),
             ],
             compiler_params=pltpu.CompilerParams(

time: 45.4 us -> 40.5 us (0.89)
  Pallas kernels: 44.7 us -> 39.7 us
    pallas_call x1, Pallas kernels: 44 us -> 39 us  [local(): pl.pallas_call(lambda *refs: kernel(nx, n, *refs), out_shape=shapes, in_s...]
where the time goes in v3:
time: 40.5 us; the launch traced here: 40.4 us
  Pallas kernels  39.7 us (98%)
  between operations  0.64 us (2%)
    pallas_call x1, Pallas kernels, local(): pl.pallas_call(lambda *refs: kernel(nx, n, *refs), out_shape=shapes, in_s...  39 us

profile of v3, /device:TPU:1, one launch (start us, length us, event | category | flops | bytes accessed | tf_op | source)
XLA Modules:
  0.0 40.4 jit_solution(3482888880293314086)
XLA Ops:
  0.6 39.0 %shard_map.41 = (f32[8,16,128]{2,1,0:T(8,128)S(1)}, f32[19,4,2,256]{3,2,1,0:T(2,128)S(1)}) custom-call(f32[8,16,128]{2,1,0:T(8,128)} %refs_0_.1, f32[19,4,2,256]{3,2,1,0:T(2,128)} %refs_1_.1), custom_call_target="tpu_custom_call" | custom-call | tf_op jit(solution)/shard_map/pallas_call | solution.py:521
  39.7 0.7 %shard_map.42 = (f32[8,16,128]{2,1,0:T(8,128)}, f32[19,4,2,256]{3,2,1,0:T(2,128)}) custom-call(f32[8,16,128]{2,1,0:T(8,128)S(1)} %get-tuple-element.4.dens, f32[19,4,2,256]{3,2,1,0:T(2,128)S(1)} %get-tuple-element.5.pops), custom_call_target="tpu_custom_call" | custom-call | tf_op jit(solution)/shard_map/pallas_call | solution.py:544

commit v4 on v3

v4 whole, which is shorter than its diff:
```python
import jax
import jax.numpy as jnp
from jax import lax
from jax.experimental import pallas as pl
from jax.experimental.pallas import tpu as pltpu
from jax.sharding import PartitionSpec as P

MESH = pl.DeviceIdType.MESH
EXACT = lax.Precision.HIGHEST
F32 = jnp.float32

TIME_STEP = 0.0008
FORCE_UNIT = 0.005
SPEED_UNIT = 2000.0
RELAX_TIME = 0.8
QUENCH = -0.25

SPEEDS = [
    (0, 0, 0),
    (1, 0, 0), (-1, 0, 0), (0, 1, 0), (0, -1, 0), (0, 0, 1), (0, 0, -1),
    (1, 1, 0), (-1, -1, 0), (1, -1, 0), (-1, 1, 0),
    (1, 0, 1), (-1, 0, -1), (1, 0, -1), (-1, 0, 1),
    (0, 1, 1), (0, -1, -1), (0, 1, -1), (0, -1, 1),
]
WEIGHTS = [1.0 / 3.0] + [1.0 / 18.0] * 6 + [1.0 / 36.0] * 12

MASS = 19
FIELDS = 23
RISE_X = [q for q in range(19) if SPEEDS[q][0] == 1]
FALL_X = [q for q in range(19) if SPEEDS[q][0] == -1]
RISE_Z = [q for q in range(19) if SPEEDS[q][2] == 1]
FALL_Z = [q for q in range(19) if SPEEDS[q][2] == -1]
MOMENTS = [MASS, MASS + 1, MASS + 2, MASS + 3]
DIAGONALS = [(1, 1), (1, -1), (-1, 1), (-1, -1)]


def dot_t(a, b):
    return lax.dot_general(
        a, b, (((1,), (1,)), ((), ())), precision=EXACT, preferred_element_type=F32
    )


def t_dot(a, b):
    return lax.dot_general(
        a, b, (((0,), (0,)), ((), ())), precision=EXACT, preferred_element_type=F32
    )


def iota(shape, dim):
    return lax.broadcasted_iota(jnp.int32, shape, dim)


def kernel(
    nx, n, dens_hbm, pops_hbm, OD, OP,
    E, E1, L1, PT, FA, FB, SP, SF, RF, SM, RM, MQ, MX, PV, EP, XS, XR, ZS, ZR, DS, DR, FR, RS,
    dsem, psem, h1_s, h1_r, h2_s, h2_r, px_s, px_r, pz_s, pz_r, pd_s, pd_r,
    ms_s, ms_r, fs_s, fs_r,
):
    L = 4 * n
    gx = lax.axis_index("gx")
    gy = lax.axis_index("gy")

    def place(sx, sy):
        return {"gx": lax.rem(gx + sx + nx, nx), "gy": lax.rem(gy + sy + n, n)}

    barrier = pltpu.get_barrier_semaphore()
    for sx, sy in DIAGONALS + [(1, 0), (-1, 0)]:
        pl.semaphore_signal(barrier, inc=1, device_id=place(sx, sy), device_id_type=MESH)

    @pl.loop(1, n)
    def _(k):
        pl.semaphore_signal(barrier, inc=1, device_id=place(0, k), device_id_type=MESH)

    dens_in = pltpu.make_async_copy(dens_hbm, E.at[pl.ds(5, 8), pl.ds(8, 16)], dsem)
    dens_in.start()
    pops_in = pltpu.make_async_copy(pops_hbm, PV, psem)
    pops_in.start()

    def remote(src, dst, send, recv, where):
        return pltpu.make_async_remote_copy(
            src_ref=src, dst_ref=dst, send_sem=send, recv_sem=recv, device_id=where,
            device_id_type=MESH,
        )

    lane = iota((1, L), 1)

    pops_in.wait()
    for h in range(2):
        for member in range(19):
            for x in range(4):
                EP[h, member, pl.ds(x * 4 + 5, 2), :] = PV[member, x, :, pl.ds(h * L, L)]
        total = jnp.zeros((24, L), F32)
        moment = [jnp.zeros((24, L), F32) for _ in range(3)]
        for member in range(19):
            value = EP[h, member]
            total = total + value
            for c in range(3):
                if SPEEDS[member][c] == 1:
                    moment[c] = moment[c] + value
                elif SPEEDS[member][c] == -1:
                    moment[c] = moment[c] - value
        EP[h, MASS] = total
        for c in range(3):
            EP[h, MASS + 1 + c] = moment[c]

    for way, (members, row) in enumerate(((RISE_X, 17), (FALL_X, 5))):
        for f, field in enumerate(members + MOMENTS):
            for h in range(2):
                XS[way, f * 2 + h] = EP[h, field, pl.ds(row, 2), :]
    for way, (members, zi) in enumerate(((RISE_Z, 2), (FALL_Z, 1))):
        for f, field in enumerate(members + MOMENTS):
            for h in range(2):
                ZS[way, f * 2 + h] = EP[h, field, pl.ds(4 + zi, 4, stride=4), :]
    spread = [
        jnp.where((iota((n, L), 1) + h * L) // 8 == iota((n, L), 0), 1.0, 0.0).astype(F32)
        for h in range(2)
    ]
    for zl in range(2):
        result = None
        for h in range(2):
            for c in range(4):
                MX[zl, h, pl.ds(c * 4, 4), :] = EP[h, MASS + c, pl.ds(5 + zl, 4, stride=4), :]
            values = MX[zl, h]
            tiles = jnp.concatenate(
                [jnp.where(lax.rem(lane, 8) == y, values, 0.0) for y in range(8)], axis=0
            )
            part = dot_t(spread[h], tiles)
            result = part if result is None else result + part
        SM[pl.ds(zl, n, stride=8), :] = result

    dens_in.wait()
    pl.semaphore_wait(barrier, n + 5)

    def boxes(buf, items, send, recv):
        copies = []
        for i, (where, x0, x1, xs, y0, y1, ys) in enumerate(items):
            copies.append(remote(
                buf.at[pl.ds(x0, xs), pl.ds(y0, ys)], buf.at[pl.ds(x1, xs), pl.ds(y1, ys)],
                send.at[i], recv.at[i], place(*where),
            ))
        for copy in copies:
            copy.start()
        return copies

    def around(width, corner, rows):
        lo, hi = width, width + 8
        return [
            ((sx, sy),
             *((hi - corner, lo - corner, corner) if sx == 1 else (lo, hi, corner)),
             *((24 - rows, 8 - rows, rows) if sy == 1 else (8, 24, rows)))
            for sx, sy in DIAGONALS
        ] + [
            ((1, 0), hi - width, 0, width, 8, 8, 16),
            ((-1, 0), lo, hi, width, 8, 8, 16),
            ((0, 1), lo, lo, 8, 21, 5, 3),
            ((0, -1), lo, lo, 8, 8, 24, 3),
        ]

    def others():
        if n % 32:
            return [lax.rem(gy + k, n) for k in range(1, n)]
        z, inner = gy // 8, lax.rem(gy, 8)
        groups = (3 - z, lax.rem(z + 2, 4), z + 1 - 2 * lax.rem(z, 2), z)
        return [
            to_z * 8 + lax.rem(inner + k, 8)
            for i, to_z in enumerate(groups) for k in range(1 if i == 3 else 0, 8)
        ]

    def to_all(src, dst, rows, send, recv):
        for to in others():
            remote(
                src.at[pl.ds(pl.multiple_of(to * 8, 8), rows)],
                dst.at[pl.ds(pl.multiple_of(gy * 8, 8), rows)],
                send, recv, {"gx": gx, "gy": to},
            ).start()
        for slot in range(rows):
            dst[pl.ds(gy * 8 + slot, 1), :] = src[pl.ds(gy * 8 + slot, 1), :]

    def wait_all(buf, rows, sem):
        whole = buf.at[pl.ds(0, (n - 1) * rows)]
        pltpu.make_async_copy(whole, whole, sem).wait()

    halo = boxes(E, around(5, 4, 3), h1_s, h1_r)
    to_all(SM, RM, 2, ms_s, ms_r)
    face_x = [
        remote(XS.at[0], XR.at[0], px_s.at[0], px_r.at[0], place(1, 0)),
        remote(XS.at[1], XR.at[1], px_s.at[1], px_r.at[1], place(-1, 0)),
    ]
    face_z = [
        remote(ZS.at[0], ZR.at[0], pz_s.at[0], pz_r.at[0], place(0, 1)),
        remote(ZS.at[1], ZR.at[1], pz_s.at[1], pz_r.at[1], place(0, -1)),
    ]
    for copy in face_x + face_z:
        copy.start()

    def turn(value, by):
        return pltpu.roll(value, by % L, 1)

    def lap(ref, i, r0, rows):
        c = ref[i, pl.ds(r0, rows), :]
        return c, (
            -6.0 * c + ref[i - 1, pl.ds(r0, rows), :] + ref[i + 1, pl.ds(r0, rows), :]
            + ref[i, pl.ds(r0 - 1, rows), :] + ref[i, pl.ds(r0 + 1, rows), :]
            + turn(c, 1) + turn(c, -1)
        )

    def potential(src, first, layers, r0, rows):
        for i in range(layers + 2):
            L1[i, pl.ds(0, rows), :] = lap(src, first + i + 1, r0, rows)[1]
        for j in range(layers):
            c, second = lap(L1, j + 1, 1, rows)
            rho = src[first + j + 2, pl.ds(r0 + 1, rows), :]
            PT[j, pl.ds(0, rows), :] = (
                (QUENCH + 1.0) * rho + 2.0 * c + second + rho * rho * rho
            )

    for copy in halo:
        copy.wait_recv()
    potential(E, 0, 14, 6, 24)

    scale = -0.5 * FORCE_UNIT * 0.125
    zeros = jnp.zeros((16, L), F32)
    for extra in range(8, 16):
        FB[pl.ds(extra, 16, stride=16), :] = zeros

    def force_pair(src, e0, p0, r0, rows):
        sums = [None, None, None]
        for k in range(2):
            rho = src[e0 + k, pl.ds(r0, rows), :] * scale
            mid = PT[p0 + k, pl.ds(1, rows), :]
            parts = (
                PT[p0 + k + 1, pl.ds(1, rows), :] - PT[p0 + k - 1, pl.ds(1, rows), :],
                PT[p0 + k, pl.ds(2, rows), :] - PT[p0 + k, pl.ds(0, rows), :],
                turn(mid, -1) - turn(mid, 1),
            )
            for c in range(3):
                value = rho * parts[c]
                sums[c] = value if sums[c] is None else sums[c] + value
        return sums

    for xi in range(6):
        sums = force_pair(E, 2 * xi + 3, 2 * xi + 1, 8, 16)
        for c in range(3):
            cx = c * 6 + xi
            if 1 <= xi <= 4:
                SP[c * 4 + xi - 1] = sums[c]
            if cx < 16:
                FA[pl.ds(cx, 16, stride=16), :] = sums[c]
            else:
                for zl in range(4):
                    FB[pl.ds((cx - 16) * 4 + zl, 16, stride=16), :] = turn(
                        sums[c], -2 * (zl - 1)
                    )
    shape = (4 * n, L)
    row = iota(shape, 0)
    window = lax.rem(2 * lax.rem(row, n) - 1 + row // n + 2 * n, 2 * n)
    choose = jnp.where(iota(shape, 1) // 2 == window, 1.0, 0.0).astype(F32)
    ga = jnp.concatenate(
        [FA[pl.ds(32 * y, 16), :] + FA[pl.ds(32 * y + 16, 16), :] for y in range(8)], axis=0
    )
    gb = jnp.concatenate(
        [FB[pl.ds(32 * y, 16), :] + FB[pl.ds(32 * y + 16, 16), :] for y in range(8)], axis=0
    )
    ta = dot_t(choose, ga)
    tb = dot_t(choose[n:2 * n], gb)
    for zl in range(4):
        SF[pl.ds(zl, n, stride=8), :] = ta[zl * n:(zl + 1) * n]
    SF[pl.ds(4, n, stride=8), :] = tb

    to_all(SF, RF, 5, fs_s, fs_r)

    wait_all(RM, 2, ms_r)
    shape = (2 * n, L)
    row = iota(shape, 0)
    pick = iota(shape, 1) // 2 == 2 * lax.rem(row, n) + row // n
    both = jnp.concatenate([RM[pl.ds(zl, n, stride=8), :] for zl in range(2)], axis=0)
    wide = t_dot(both, jnp.where(pick, 1.0, 0.0).astype(F32))
    for y in range(16):
        MQ[pl.ds(y * 16, 16), :] = wide[(y // 2) * 16:(y // 2 + 1) * 16]

    even_y = lax.rem(iota((16, L), 0), 2) == 0
    even_z = lax.rem(iota((16, L), 1), 2) == 0

    def fine_speed(x):
        mass = MQ[pl.ds(x, 16, stride=16), :]
        inverse = SPEED_UNIT * 0.5 / mass
        out = []
        for c in range(3):
            s = SP[c * 4 + x]
            s = s + jnp.where(even_y, pltpu.roll(s, 15, 0), pltpu.roll(s, 1, 0))
            s = s + jnp.where(even_z, turn(s, -1), turn(s, 1))
            m = MQ[pl.ds((c + 1) * 4 + x, 16, stride=16), :]
            out.append((m + 0.5 * s) * inverse)
        return out

    def advance(src, e, p, speed):
        mid = src[e, pl.ds(8, 16), :]
        advect = (
            speed[0] * (src[e + 1, pl.ds(8, 16), :] - src[e - 1, pl.ds(8, 16), :])
            + speed[1] * (src[e, pl.ds(9, 16), :] - src[e, pl.ds(7, 16), :])
            + speed[2] * (turn(mid, -1) - turn(mid, 1))
        )
        return mid + TIME_STEP * (lap(PT, p, 1, 16)[1] - advect)

    for x in range(4):
        speed = fine_speed(x)
        for c in range(3):
            SP[c * 4 + x] = speed[c]
        for k in (2 * x, 2 * x + 1):
            E1[k + 3, pl.ds(8, 16), :] = advance(E, k + 5, k + 3, speed)
    again = boxes(E1, around(3, 2, 2), h2_s, h2_r)

    for way in range(2):
        face_x[way].wait_recv()
    for way in range(2):
        for side, members in enumerate((RISE_X, FALL_X)):
            member = SPEEDS.index((1 - 2 * side, 0, 1 - 2 * way))
            for f, item in enumerate([members.index(member), 5, 6, 7, 8]):
                for h in range(2):
                    both = XR[side, item * 2 + h]
                    DS[way, pl.ds((side * 5 + f) * 2 + h, 1), :] = both[1 - way:2 - way]
    edges = [
        remote(DS.at[0], DR.at[0], pd_s.at[0], pd_r.at[0], place(0, 1)),
        remote(DS.at[1], DR.at[1], pd_s.at[1], pd_r.at[1], place(0, -1)),
    ]
    for copy in edges:
        copy.start()
    for way, (members, row) in enumerate(((RISE_X, 1), (FALL_X, 21))):
        for f, field in enumerate(members + MOMENTS):
            for h in range(2):
                EP[h, field, pl.ds(row, 2), :] = XR[way, f * 2 + h]
    for way, (members, zi) in enumerate(((RISE_Z, 0), (FALL_Z, 3))):
        face_z[way].wait_recv()
        for f, field in enumerate(members + MOMENTS):
            for h in range(2):
                EP[h, field, pl.ds(4 + zi, 4, stride=4), :] = ZR[way, f * 2 + h]
    for way in range(2):
        edges[way].wait_recv()
        for side in range(2):
            row = side * 20 + way * 3
            member = SPEEDS.index((1 - 2 * side, 0, 1 - 2 * way))
            for f, field in enumerate([member] + MOMENTS):
                for h in range(2):
                    EP[h, field, pl.ds(row, 1), :] = DR[way, pl.ds((side * 5 + f) * 2 + h, 1), :]

    wait_all(RF, 5, fs_r)
    half = n // 2
    expand = jnp.where(iota((half, L), 1) // 8 == iota((half, L), 0), 1.0, 0.0).astype(F32)
    for slot in range(5):
        whole = RF[pl.ds(slot, n, stride=8), :]
        for h in range(2):
            q = t_dot(whole[h * half:(h + 1) * half], expand)
            value = q[0:16]
            for y in range(1, 8):
                value = jnp.where(lax.rem(lane, 8) == y, q[y * 16:(y + 1) * 16], value)
            if slot < 4:
                FR[h, pl.ds(slot, 16, stride=4), :] = value
            else:
                FR[h, pl.ds(64, 16), :] = value

    state = []
    for h in range(2):
        mass = EP[h, MASS]
        inverse = 1.0 / mass
        force = [FR[h, pl.ds(c * 24, 24), :] for c in range(3)]
        flow = [(EP[h, MASS + 1 + c] + 0.5 * force[c]) * inverse for c in range(3)]
        square = flow[0] * flow[0] + flow[1] * flow[1] + flow[2] * flow[2]
        work = flow[0] * force[0] + flow[1] * force[1] + flow[2] * force[2]
        state.append((mass, force, flow, 1.0 - 1.5 * square, work))
    rate = 1.0 / RELAX_TIME
    gain = 1.0 - 0.5 / RELAX_TIME

    def along(speed, vector):
        out = None
        for c in range(3):
            if speed[c] == 1:
                out = vector[c] if out is None else out + vector[c]
            elif speed[c] == -1:
                out = -vector[c] if out is None else out - vector[c]
        return out

    for member in range(19):
        cx, cy, cz = SPEEDS[member]
        w = WEIGHTS[member]
        parts = []
        for h in range(2):
            mass, force, flow, rest, work = state[h]
            p = EP[h, member]
            if member == 0:
                new = (rate * w) * mass * rest - (3.0 * gain * w) * work
            else:
                cu, cf = along(SPEEDS[member], flow), along(SPEEDS[member], force)
                new = (rate * w) * mass * (rest + cu * (3.0 + 4.5 * cu)) + (gain * w) * (
                    3.0 * (cf - work) + 9.0 * cu * cf
                )
            parts.append(p * (1.0 - rate) + new)
        if cy:
            turned = [pltpu.roll(v, cy % L, 1) for v in parts]
            edge = lane == (0 if cy == 1 else L - 1)
            parts = [jnp.where(edge, turned[1 - h], turned[h]) for h in range(2)]
        for h in range(2):
            RS[member, h] = parts[h]
            for x in range(4):
                OP[member, x, :, pl.ds(h * L, L)] = RS[
                    member, h, pl.ds((x + 1 - cx) * 4 + 1 - cz, 2), :
                ]

    for copy in again:
        copy.wait_recv()
    potential(E1, 0, 10, 6, 24)
    for x in range(4):
        speed = [SP[c * 4 + x] for c in range(3)]
        for k in (2 * x, 2 * x + 1):
            OD[k] = advance(E1, k + 3, k + 1, speed)

    for copy in halo + again + face_x + face_z + edges:
        copy.wait_send()
    wait_all(SM, 2, ms_s)
    wait_all(SF, 5, fs_s)


def put(dens, pops, dens_out, pops_out, dsem, psem):
    first = pltpu.make_async_copy(dens, dens_out, dsem)
    second = pltpu.make_async_copy(pops, pops_out, psem)
    second.start()
    first.start()
    first.wait()
    second.wait()


def solution(mesh):
    nx, n = mesh.shape["gx"], mesh.shape["gy"]
    L = 4 * n

    def local(density, populations):
        vmem = lambda *shape: pltpu.VMEM(shape, F32)
        dma = lambda *shape: pltpu.SemaphoreType.DMA(shape)
        any_spec = pl.BlockSpec(memory_space=pl.ANY)
        vmem_spec = pl.BlockSpec(memory_space=pltpu.VMEM)
        shapes = (
            jax.ShapeDtypeStruct((8, 16, L), F32),
            jax.ShapeDtypeStruct((19, 4, 2, 2 * L), F32),
        )
        density = pltpu.with_memory_space_constraint(density, pltpu.HBM)
        populations = pltpu.with_memory_space_constraint(populations, pltpu.HBM)
        density, populations = pl.pallas_call(
            lambda *refs: kernel(nx, n, *refs),
            out_shape=shapes,
            in_specs=[any_spec, any_spec],
            out_specs=(vmem_spec, vmem_spec),
            scratch_shapes=[
                vmem(18, 32, L), vmem(14, 32, L), vmem(16, 32, L), vmem(14, 32, L),
                vmem(256, L), vmem(256, L), vmem(12, 16, L),
                vmem(n * 8, 128), vmem(n * 8, 128), vmem(n * 8, 128), vmem(n * 8, 128),
                vmem(256, L), vmem(2, 2, 16, L), vmem(19, 4, 2, 2 * L),
                vmem(2, FIELDS, 24, L), vmem(2, 18, 2, L), vmem(2, 18, 2, L),
                vmem(2, 18, 4, L), vmem(2, 18, 4, L), vmem(2, 24, L), vmem(2, 24, L),
                vmem(2, 80, L), vmem(19, 2, 24, L),
                dma(), dma(),
                dma(8), dma(8), dma(8), dma(8),
                dma(2), dma(2), dma(2), dma(2), dma(2), dma(2),
                dma(), dma(), dma(), dma(),
            ],
            compiler_params=pltpu.CompilerParams(
                collective_id=0, has_side_effects=True, vmem_limit_bytes=16 * 2**20
            ),
        )(density, populations)
        return pl.pallas_call(
            put,
            out_shape=shapes,
            in_specs=[any_spec, any_spec],
            out_specs=(any_spec, any_spec),
            scratch_shapes=[dma(), dma()],
            compiler_params=pltpu.CompilerParams(vmem_limit_bytes=8 * 2**20),
        )(density, populations)

    return jax.shard_map(
        local,
        mesh=mesh,
        in_specs=(P("gx", "gy", None), P(None, "gx", "gy", None)),
        out_specs=(P("gx", "gy", None), P(None, "gx", "gy", None)),
        check_vma=False,
    )
```

time: 40.5 us -> 37.2 us (0.919)
  Pallas kernels: 39.7 us -> 36.4 us
    pallas_call x1, Pallas kernels: 39 us -> 35.7 us  [local(): pl.pallas_call(lambda *refs: kernel(nx, n, *refs), out_shape=shapes, in_s...]
where the time goes in v4:
time: 37.2 us; the launch traced here: 37 us
  Pallas kernels  36.4 us (98%)
  between operations  0.64 us (2%)
    pallas_call x1, Pallas kernels, local(): pl.pallas_call(lambda *refs: kernel(nx, n, *refs), out_shape=shapes, in_s...  35.7 us

profile of v4, /device:TPU:1, one launch (start us, length us, event | category | flops | bytes accessed | tf_op | source)
XLA Modules:
  0.0 37.0 jit_solution(11297246695900711428)
XLA Ops:
  0.6 35.7 %shard_map.41 = (f32[8,16,128]{2,1,0:T(8,128)S(1)}, f32[19,4,2,256]{3,2,1,0:T(2,128)S(1)}) custom-call(f32[8,16,128]{2,1,0:T(8,128)} %refs_0_.1, f32[19,4,2,256]{3,2,1,0:T(2,128)} %refs_1_.1), custom_call_target="tpu_custom_call" | custom-call | tf_op jit(solution)/shard_map/pallas_call | solution.py:446
  36.3 0.7 %shard_map.42 = (f32[8,16,128]{2,1,0:T(8,128)}, f32[19,4,2,256]{3,2,1,0:T(2,128)}) custom-call(f32[8,16,128]{2,1,0:T(8,128)S(1)} %get-tuple-element.4.dens, f32[19,4,2,256]{3,2,1,0:T(2,128)S(1)} %get-tuple-element.5.pops), custom_call_target="tpu_custom_call" | custom-call | tf_op jit(solution)/shard_map/pallas_call | solution.py:468

commit v5 on v4

--- a/solution.py
+++ b/solution.py
@@ -64,7 +64,7 @@
         return {"gx": lax.rem(gx + sx + nx, nx), "gy": lax.rem(gy + sy + n, n)}
 
     barrier = pltpu.get_barrier_semaphore()
-    for sx, sy in DIAGONALS + [(1, 0), (-1, 0)]:
+    for sx, sy in ((1, 0), (-1, 0)):
         pl.semaphore_signal(barrier, inc=1, device_id=place(sx, sy), device_id_type=MESH)
 
     @pl.loop(1, n)
@@ -129,32 +129,18 @@
         SM[pl.ds(zl, n, stride=8), :] = result
 
     dens_in.wait()
-    pl.semaphore_wait(barrier, n + 5)
-
-    def boxes(buf, items, send, recv):
+    pl.semaphore_wait(barrier, n + 1)
+
+    def boxes(buf, items, first, send, recv):
         copies = []
         for i, (where, x0, x1, xs, y0, y1, ys) in enumerate(items):
             copies.append(remote(
                 buf.at[pl.ds(x0, xs), pl.ds(y0, ys)], buf.at[pl.ds(x1, xs), pl.ds(y1, ys)],
-                send.at[i], recv.at[i], place(*where),
+                send.at[first + i], recv.at[first + i], place(*where),
             ))
         for copy in copies:
             copy.start()
         return copies
-
-    def around(width, corner, rows):
-        lo, hi = width, width + 8
-        return [
-            ((sx, sy),
-             *((hi - corner, lo - corner, corner) if sx == 1 else (lo, hi, corner)),
-             *((24 - rows, 8 - rows, rows) if sy == 1 else (8, 24, rows)))
-            for sx, sy in DIAGONALS
-        ] + [
-            ((1, 0), hi - width, 0, width, 8, 8, 16),
-            ((-1, 0), lo, hi, width, 8, 8, 16),
-            ((0, 1), lo, lo, 8, 21, 5, 3),
-            ((0, -1), lo, lo, 8, 8, 24, 3),
-        ]
 
     def others():
         if n % 32:
@@ -180,18 +166,57 @@
         whole = buf.at[pl.ds(0, (n - 1) * rows)]
         pltpu.make_async_copy(whole, whole, sem).wait()
 
-    halo = boxes(E, around(5, 4, 3), h1_s, h1_r)
+    near = boxes(
+        E, [((1, 0), 10, 2, 3, 8, 8, 16), ((-1, 0), 5, 13, 3, 8, 8, 16)], 0, h1_s, h1_r
+    )
+    rows = boxes(
+        E, [((0, 1), 5, 5, 8, 21, 5, 3), ((0, -1), 5, 5, 8, 8, 24, 3)], 2, h1_s, h1_r
+    )
+    far = boxes(
+        E, [((1, 0), 8, 0, 2, 8, 8, 16), ((-1, 0), 8, 16, 2, 8, 8, 16)], 4, h1_s, h1_r
+    )
     to_all(SM, RM, 2, ms_s, ms_r)
+    face_z = [
+        remote(ZS.at[0], ZR.at[0], pz_s.at[0], pz_r.at[0], place(0, 1)),
+        remote(ZS.at[1], ZR.at[1], pz_s.at[1], pz_r.at[1], place(0, -1)),
+    ]
     face_x = [
         remote(XS.at[0], XR.at[0], px_s.at[0], px_r.at[0], place(1, 0)),
         remote(XS.at[1], XR.at[1], px_s.at[1], px_r.at[1], place(-1, 0)),
     ]
-    face_z = [
-        remote(ZS.at[0], ZR.at[0], pz_s.at[0], pz_r.at[0], place(0, 1)),
-        remote(ZS.at[1], ZR.at[1], pz_s.at[1], pz_r.at[1], place(0, -1)),
+    for copy in face_z + face_x:
+        copy.start()
+
+    for copy in rows:
+        copy.wait_recv()
+    corners = boxes(
+        E,
+        [
+            (where, x0, x1, 4, y0, y0, 3)
+            for where, x0, x1 in (((1, 0), 9, 1), ((-1, 0), 5, 13)) for y0 in (5, 24)
+        ],
+        6, h1_s, h1_r,
+    )
+    for way in range(2):
+        face_z[way].wait_recv()
+    for way, (sx, x) in enumerate(((1, 3), (-1, 0))):
+        for side, members in enumerate((RISE_Z, FALL_Z)):
+            member = SPEEDS.index((sx, 0, 1 - 2 * side))
+            for f, item in enumerate([members.index(member), 5, 6, 7, 8]):
+                for h in range(2):
+                    DS[way, pl.ds((side * 5 + f) * 2 + h, 1), :] = ZR[
+                        side, item * 2 + h, pl.ds(x, 1), :
+                    ]
+    edges = [
+        remote(DS.at[0], DR.at[0], pd_s.at[0], pd_r.at[0], place(1, 0)),
+        remote(DS.at[1], DR.at[1], pd_s.at[1], pd_r.at[1], place(-1, 0)),
     ]
-    for copy in face_x + face_z:
+    for copy in edges:
         copy.start()
+    for way, (members, zi) in enumerate(((RISE_Z, 0), (FALL_Z, 3))):
+        for f, field in enumerate(members + MOMENTS):
+            for h in range(2):
+                EP[h, field, pl.ds(4 + zi, 4, stride=4), :] = ZR[way, f * 2 + h]
 
     def turn(value, by):
         return pltpu.roll(value, by % L, 1)
@@ -204,19 +229,28 @@
             + turn(c, 1) + turn(c, -1)
         )
 
-    def potential(src, first, layers, r0, rows):
-        for i in range(layers + 2):
-            L1[i, pl.ds(0, rows), :] = lap(src, first + i + 1, r0, rows)[1]
-        for j in range(layers):
+    def potential(src, outer, inner, r0, rows):
+        for i in outer:
+            L1[i, pl.ds(0, rows), :] = lap(src, i + 1, r0, rows)[1]
+        for j in inner:
             c, second = lap(L1, j + 1, 1, rows)
-            rho = src[first + j + 2, pl.ds(r0 + 1, rows), :]
+            rho = src[j + 2, pl.ds(r0 + 1, rows), :]
             PT[j, pl.ds(0, rows), :] = (
                 (QUENCH + 1.0) * rho + 2.0 * c + second + rho * rho * rho
             )
 
-    for copy in halo:
+    wait_all(RM, 2, ms_r)
+    shape = (2 * n, L)
+    row = iota(shape, 0)
+    pick = iota(shape, 1) // 2 == 2 * lax.rem(row, n) + row // n
+    both = jnp.concatenate([RM[pl.ds(zl, n, stride=8), :] for zl in range(2)], axis=0)
+    wide = t_dot(both, jnp.where(pick, 1.0, 0.0).astype(F32))
+    for y in range(16):
+        MQ[pl.ds(y * 16, 16), :] = wide[(y // 2) * 16:(y // 2 + 1) * 16]
+
+    for copy in near + corners:
         copy.wait_recv()
-    potential(E, 0, 14, 6, 24)
+    potential(E, range(2, 14), range(2, 12), 6, 24)
 
     scale = -0.5 * FORCE_UNIT * 0.125
     zeros = jnp.zeros((16, L), F32)
@@ -238,7 +272,7 @@
                 sums[c] = value if sums[c] is None else sums[c] + value
         return sums
 
-    for xi in range(6):
+    def outgoing(xi):
         sums = force_pair(E, 2 * xi + 3, 2 * xi + 1, 8, 16)
         for c in range(3):
             cx = c * 6 + xi
@@ -251,32 +285,9 @@
                     FB[pl.ds((cx - 16) * 4 + zl, 16, stride=16), :] = turn(
                         sums[c], -2 * (zl - 1)
                     )
-    shape = (4 * n, L)
-    row = iota(shape, 0)
-    window = lax.rem(2 * lax.rem(row, n) - 1 + row // n + 2 * n, 2 * n)
-    choose = jnp.where(iota(shape, 1) // 2 == window, 1.0, 0.0).astype(F32)
-    ga = jnp.concatenate(
-        [FA[pl.ds(32 * y, 16), :] + FA[pl.ds(32 * y + 16, 16), :] for y in range(8)], axis=0
-    )
-    gb = jnp.concatenate(
-        [FB[pl.ds(32 * y, 16), :] + FB[pl.ds(32 * y + 16, 16), :] for y in range(8)], axis=0
-    )
-    ta = dot_t(choose, ga)
-    tb = dot_t(choose[n:2 * n], gb)
-    for zl in range(4):
-        SF[pl.ds(zl, n, stride=8), :] = ta[zl * n:(zl + 1) * n]
-    SF[pl.ds(4, n, stride=8), :] = tb
-
-    to_all(SF, RF, 5, fs_s, fs_r)
-
-    wait_all(RM, 2, ms_r)
-    shape = (2 * n, L)
-    row = iota(shape, 0)
-    pick = iota(shape, 1) // 2 == 2 * lax.rem(row, n) + row // n
-    both = jnp.concatenate([RM[pl.ds(zl, n, stride=8), :] for zl in range(2)], axis=0)
-    wide = t_dot(both, jnp.where(pick, 1.0, 0.0).astype(F32))
-    for y in range(16):
-        MQ[pl.ds(y * 16, 16), :] = wide[(y // 2) * 16:(y // 2 + 1) * 16]
+
+    for xi in range(1, 5):
+        outgoing(xi)
 
     even_y = lax.rem(iota((16, L), 0), 2) == 0
     even_z = lax.rem(iota((16, L), 1), 2) == 0
@@ -308,37 +319,56 @@
             SP[c * 4 + x] = speed[c]
         for k in (2 * x, 2 * x + 1):
             E1[k + 3, pl.ds(8, 16), :] = advance(E, k + 5, k + 3, speed)
-    again = boxes(E1, around(3, 2, 2), h2_s, h2_r)
+    again = boxes(
+        E1,
+        [
+            ((sx, sy), *((9, 1, 2) if sx == 1 else (3, 11, 2)),
+             *((22, 6, 2) if sy == 1 else (8, 24, 2)))
+            for sx, sy in DIAGONALS
+        ] + [
+            ((1, 0), 8, 0, 3, 8, 8, 16),
+            ((-1, 0), 3, 11, 3, 8, 8, 16),
+            ((0, 1), 3, 3, 8, 21, 5, 3),
+            ((0, -1), 3, 3, 8, 8, 24, 3),
+        ],
+        0, h2_s, h2_r,
+    )
+
+    for copy in far:
+        copy.wait_recv()
+    potential(E, (0, 1, 14, 15), (0, 1, 12, 13), 6, 24)
+    for xi in (0, 5):
+        outgoing(xi)
+
+    shape = (4 * n, L)
+    row = iota(shape, 0)
+    window = lax.rem(2 * lax.rem(row, n) - 1 + row // n + 2 * n, 2 * n)
+    choose = jnp.where(iota(shape, 1) // 2 == window, 1.0, 0.0).astype(F32)
+    ga = jnp.concatenate(
+        [FA[pl.ds(32 * y, 16), :] + FA[pl.ds(32 * y + 16, 16), :] for y in range(8)], axis=0
+    )
+    gb = jnp.concatenate(
+        [FB[pl.ds(32 * y, 16), :] + FB[pl.ds(32 * y + 16, 16), :] for y in range(8)], axis=0
+    )
+    ta = dot_t(choose, ga)
+    tb = dot_t(choose[n:2 * n], gb)
+    for zl in range(4):
+        SF[pl.ds(zl, n, stride=8), :] = ta[zl * n:(zl + 1) * n]
+    SF[pl.ds(4, n, stride=8), :] = tb
+
+    to_all(SF, RF, 5, fs_s, fs_r)
 
     for way in range(2):
         face_x[way].wait_recv()
-    for way in range(2):
-        for side, members in enumerate((RISE_X, FALL_X)):
-            member = SPEEDS.index((1 - 2 * side, 0, 1 - 2 * way))
-            for f, item in enumerate([members.index(member), 5, 6, 7, 8]):
-                for h in range(2):
-                    both = XR[side, item * 2 + h]
-                    DS[way, pl.ds((side * 5 + f) * 2 + h, 1), :] = both[1 - way:2 - way]
-    edges = [
-        remote(DS.at[0], DR.at[0], pd_s.at[0], pd_r.at[0], place(0, 1)),
-        remote(DS.at[1], DR.at[1], pd_s.at[1], pd_r.at[1], place(0, -1)),
-    ]
-    for copy in edges:
-        copy.start()
     for way, (members, row) in enumerate(((RISE_X, 1), (FALL_X, 21))):
         for f, field in enumerate(members + MOMENTS):
             for h in range(2):
                 EP[h, field, pl.ds(row, 2), :] = XR[way, f * 2 + h]
-    for way, (members, zi) in enumerate(((RISE_Z, 0), (FALL_Z, 3))):
-        face_z[way].wait_recv()
-        for f, field in enumerate(members + MOMENTS):
-            for h in range(2):
-                EP[h, field, pl.ds(4 + zi, 4, stride=4), :] = ZR[way, f * 2 + h]
     for way in range(2):
         edges[way].wait_recv()
-        for side in range(2):
-            row = side * 20 + way * 3
-            member = SPEEDS.index((1 - 2 * side, 0, 1 - 2 * way))
+        for side, members in enumerate((RISE_Z, FALL_Z)):
+            member = SPEEDS.index((1 - 2 * way, 0, 1 - 2 * side))
+            row = way * 20 + side * 3
             for f, field in enumerate([member] + MOMENTS):
                 for h in range(2):
                     EP[h, field, pl.ds(row, 1), :] = DR[way, pl.ds((side * 5 + f) * 2 + h, 1), :]
@@ -407,13 +437,13 @@
 
     for copy in again:
         copy.wait_recv()
-    potential(E1, 0, 10, 6, 24)
+    potential(E1, range(12), range(10), 6, 24)
     for x in range(4):
         speed = [SP[c * 4 + x] for c in range(3)]
         for k in (2 * x, 2 * x + 1):
             OD[k] = advance(E1, k + 3, k + 1, speed)
 
-    for copy in halo + again + face_x + face_z + edges:
+    for copy in near + rows + far + corners + again + face_x + face_z + edges:
         copy.wait_send()
     wait_all(SM, 2, ms_s)
     wait_all(SF, 5, fs_s)
@@ -454,10 +484,10 @@
                 vmem(n * 8, 128), vmem(n * 8, 128), vmem(n * 8, 128), vmem(n * 8, 128),
                 vmem(256, L), vmem(2, 2, 16, L), vmem(19, 4, 2, 2 * L),
                 vmem(2, FIELDS, 24, L), vmem(2, 18, 2, L), vmem(2, 18, 2, L),
-                vmem(2, 18, 4, L), vmem(2, 18, 4, L), vmem(2, 24, L), vmem(2, 24, L),
+                vmem(2, 18, 4, L), vmem(2, 18, 4, L), vmem(2, 20, L), vmem(2, 20, L),
                 vmem(2, 80, L), vmem(19, 2, 24, L),
                 dma(), dma(),
-                dma(8), dma(8), dma(8), dma(8),
+                dma(10), dma(10), dma(8), dma(8),
                 dma(2), dma(2), dma(2), dma(2), dma(2), dma(2),
                 dma(), dma(), dma(), dma(),
             ],

time: 37.2 us -> 36.3 us (0.976)
  Pallas kernels: 36.4 us -> 35.5 us
    pallas_call x1, Pallas kernels: 35.7 us -> 34.8 us  [local(): pl.pallas_call(lambda *refs: kernel(nx, n, *refs), out_shape=shapes, in_s...]
where the time goes in v5:
time: 36.3 us; the launch traced here: 36.2 us
  Pallas kernels  35.5 us (98%)
  between operations  0.64 us (2%)
    pallas_call x1, Pallas kernels, local(): pl.pallas_call(lambda *refs: kernel(nx, n, *refs), out_shape=shapes, in_s...  34.8 us

profile of v5, /device:TPU:1, one launch (start us, length us, event | category | flops | bytes accessed | tf_op | source)
XLA Modules:
  0.0 36.2 jit_solution(1201750025136051896)
XLA Ops:
  0.6 34.8 %shard_map.41 = (f32[8,16,128]{2,1,0:T(8,128)S(1)}, f32[19,4,2,256]{3,2,1,0:T(2,128)S(1)}) custom-call(f32[8,16,128]{2,1,0:T(8,128)} %refs_0_.1, f32[19,4,2,256]{3,2,1,0:T(2,128)} %refs_1_.1), custom_call_target="tpu_custom_call" | custom-call | tf_op jit(solution)/shard_map/pallas_call | solution.py:476
  35.5 0.7 %shard_map.42 = (f32[8,16,128]{2,1,0:T(8,128)}, f32[19,4,2,256]{3,2,1,0:T(2,128)}) custom-call(f32[8,16,128]{2,1,0:T(8,128)S(1)} %get-tuple-element.4.dens, f32[19,4,2,256]{3,2,1,0:T(2,128)S(1)} %get-tuple-element.5.pops), custom_call_target="tpu_custom_call" | custom-call | tf_op jit(solution)/shard_map/pallas_call | solution.py:498

commit v6 on v5

--- a/solution.py
+++ b/solution.py
@@ -248,9 +248,10 @@
     for y in range(16):
         MQ[pl.ds(y * 16, 16), :] = wide[(y // 2) * 16:(y // 2 + 1) * 16]
 
+    potential(E, range(5, 11), range(5, 9), 6, 24)
     for copy in near + corners:
         copy.wait_recv()
-    potential(E, range(2, 14), range(2, 12), 6, 24)
+    potential(E, (2, 3, 4, 11, 12, 13), (2, 3, 4, 9, 10, 11), 6, 24)
 
     scale = -0.5 * FORCE_UNIT * 0.125
     zeros = jnp.zeros((16, L), F32)
@@ -373,6 +374,14 @@
                 for h in range(2):
                     EP[h, field, pl.ds(row, 1), :] = DR[way, pl.ds((side * 5 + f) * 2 + h, 1), :]
 
+    for copy in again:
+        copy.wait_recv()
+    potential(E1, range(12), range(10), 6, 24)
+    for x in range(4):
+        speed = [SP[c * 4 + x] for c in range(3)]
+        for k in (2 * x, 2 * x + 1):
+            OD[k] = advance(E1, k + 3, k + 1, speed)
+
     wait_all(RF, 5, fs_r)
     half = n // 2
     expand = jnp.where(iota((half, L), 1) // 8 == iota((half, L), 0), 1.0, 0.0).astype(F32)
@@ -388,6 +397,8 @@
             else:
                 FR[h, pl.ds(64, 16), :] = value
 
+    rate = 1.0 / RELAX_TIME
+    gain = 1.0 - 0.5 / RELAX_TIME
     state = []
     for h in range(2):
         mass = EP[h, MASS]
@@ -396,9 +407,8 @@
         flow = [(EP[h, MASS + 1 + c] + 0.5 * force[c]) * inverse for c in range(3)]
         square = flow[0] * flow[0] + flow[1] * flow[1] + flow[2] * flow[2]
         work = flow[0] * force[0] + flow[1] * force[1] + flow[2] * force[2]
-        state.append((mass, force, flow, 1.0 - 1.5 * square, work))
-    rate = 1.0 / RELAX_TIME
-    gain = 1.0 - 0.5 / RELAX_TIME
+        common = rate * mass * (1.0 - 1.5 * square) - (3.0 * gain) * work
+        state.append((3.0 * rate * mass, force, flow, common))
 
     def along(speed, vector):
         out = None
@@ -409,21 +419,9 @@
                 out = -vector[c] if out is None else out - vector[c]
         return out
 
-    for member in range(19):
+    def passed(member, parts):
         cx, cy, cz = SPEEDS[member]
-        w = WEIGHTS[member]
-        parts = []
-        for h in range(2):
-            mass, force, flow, rest, work = state[h]
-            p = EP[h, member]
-            if member == 0:
-                new = (rate * w) * mass * rest - (3.0 * gain * w) * work
-            else:
-                cu, cf = along(SPEEDS[member], flow), along(SPEEDS[member], force)
-                new = (rate * w) * mass * (rest + cu * (3.0 + 4.5 * cu)) + (gain * w) * (
-                    3.0 * (cf - work) + 9.0 * cu * cf
-                )
-            parts.append(p * (1.0 - rate) + new)
+        parts = [EP[h, member] * (1.0 - rate) + parts[h] for h in range(2)]
         if cy:
             turned = [pltpu.roll(v, cy % L, 1) for v in parts]
             edge = lane == (0 if cy == 1 else L - 1)
@@ -435,13 +433,23 @@
                     member, h, pl.ds((x + 1 - cx) * 4 + 1 - cz, 2), :
                 ]
 
-    for copy in again:
-        copy.wait_recv()
-    potential(E1, range(12), range(10), 6, 24)
-    for x in range(4):
-        speed = [SP[c * 4 + x] for c in range(3)]
-        for k in (2 * x, 2 * x + 1):
-            OD[k] = advance(E1, k + 3, k + 1, speed)
+    passed(0, [WEIGHTS[0] * state[h][3] for h in range(2)])
+    scaled = {}
+    for w in (WEIGHTS[1], WEIGHTS[7]):
+        scaled[w] = [(w * state[h][0], w * state[h][3]) for h in range(2)]
+    for member in range(1, 19, 2):
+        w = WEIGHTS[member]
+        plus, minus = [], []
+        for h in range(2):
+            mass, common = scaled[w][h]
+            cu, cf = along(SPEEDS[member], state[h][2]), along(SPEEDS[member], state[h][1])
+            first, second = mass * cu, (3.0 * gain * w) * cf
+            odd = first + second
+            even = common + cu * (1.5 * first + 3.0 * second)
+            plus.append(even + odd)
+            minus.append(even - odd)
+        passed(member, plus)
+        passed(member + 1, minus)
 
     for copy in near + rows + far + corners + again + face_x + face_z + edges:
         copy.wait_send()

time: 36.3 us -> 35.9 us (0.989)
  Pallas kernels: 35.5 us -> 35.1 us
    pallas_call x1, Pallas kernels: 34.8 us -> 34.4 us  [local(): pl.pallas_call(lambda *refs: kernel(nx, n, *refs), out_shape=shapes, in_s...]
where the time goes in v6:
time: 35.9 us; the launch traced here: 35.7 us
  Pallas kernels  35.1 us (98%)
  between operations  0.64 us (2%)
    pallas_call x1, Pallas kernels, local(): pl.pallas_call(lambda *refs: kernel(nx, n, *refs), out_shape=shapes, in_s...  34.4 us

profile of v6, /device:TPU:1, one launch (start us, length us, event | category | flops | bytes accessed | tf_op | source)
XLA Modules:
  0.0 35.7 jit_solution(10299045437728709665)
XLA Ops:
  0.6 34.4 %shard_map.41 = (f32[8,16,128]{2,1,0:T(8,128)S(1)}, f32[19,4,2,256]{3,2,1,0:T(2,128)S(1)}) custom-call(f32[8,16,128]{2,1,0:T(8,128)} %refs_0_.1, f32[19,4,2,256]{3,2,1,0:T(2,128)} %refs_1_.1), custom_call_target="tpu_custom_call" | custom-call | tf_op jit(solution)/shard_map/pallas_call | solution.py:484
  35.0 0.7 %shard_map.42 = (f32[8,16,128]{2,1,0:T(8,128)}, f32[19,4,2,256]{3,2,1,0:T(2,128)}) custom-call(f32[8,16,128]{2,1,0:T(8,128)S(1)} %get-tuple-element.4.dens, f32[19,4,2,256]{3,2,1,0:T(2,128)S(1)} %get-tuple-element.5.pops), custom_call_target="tpu_custom_call" | custom-call | tf_op jit(solution)/shard_map/pallas_call | solution.py:506

commit v7 on v6

--- a/solution.py
+++ b/solution.py
@@ -143,14 +143,7 @@
         return copies
 
     def others():
-        if n % 32:
-            return [lax.rem(gy + k, n) for k in range(1, n)]
-        z, inner = gy // 8, lax.rem(gy, 8)
-        groups = (3 - z, lax.rem(z + 2, 4), z + 1 - 2 * lax.rem(z, 2), z)
-        return [
-            to_z * 8 + lax.rem(inner + k, 8)
-            for i, to_z in enumerate(groups) for k in range(1 if i == 3 else 0, 8)
-        ]
+        return [lax.rem(gy + (k * (n // 2 + 1)) % n, n) for k in range(1, n)]
 
     def to_all(src, dst, rows, send, recv):
         for to in others():

time: 35.9 us -> 35.7 us (level)
  no operation moved by 1% of the time
where the time goes in v7:
time: 35.7 us; the launch traced here: 35.6 us
  Pallas kernels  35 us (98%)
  between operations  0.64 us (2%)
    pallas_call x1, Pallas kernels, local(): pl.pallas_call(lambda *refs: kernel(nx, n, *refs), out_shape=shapes, in_s...  34.3 us

profile of v7, /device:TPU:1, one launch (start us, length us, event | category | flops | bytes accessed | tf_op | source)
XLA Modules:
  0.0 35.6 jit_solution(13383047656693077247)
XLA Ops:
  0.6 34.3 %shard_map.41 = (f32[8,16,128]{2,1,0:T(8,128)S(1)}, f32[19,4,2,256]{3,2,1,0:T(2,128)S(1)}) custom-call(f32[8,16,128]{2,1,0:T(8,128)} %refs_0_.1, f32[19,4,2,256]{3,2,1,0:T(2,128)} %refs_1_.1), custom_call_target="tpu_custom_call" | custom-call | tf_op jit(solution)/shard_map/pallas_call | solution.py:477
  34.9 0.7 %shard_map.42 = (f32[8,16,128]{2,1,0:T(8,128)}, f32[19,4,2,256]{3,2,1,0:T(2,128)}) custom-call(f32[8,16,128]{2,1,0:T(8,128)S(1)} %get-tuple-element.4.dens, f32[19,4,2,256]{3,2,1,0:T(2,128)S(1)} %get-tuple-element.5.pops), custom_call_target="tpu_custom_call" | custom-call | tf_op jit(solution)/shard_map/pallas_call | solution.py:499

commit v8 on v7

--- a/solution.py
+++ b/solution.py
@@ -25,7 +25,7 @@
 WEIGHTS = [1.0 / 3.0] + [1.0 / 18.0] * 6 + [1.0 / 36.0] * 12
 
 MASS = 19
-FIELDS = 23
+FIELDS = 24
 RISE_X = [q for q in range(19) if SPEEDS[q][0] == 1]
 FALL_X = [q for q in range(19) if SPEEDS[q][0] == -1]
 RISE_Z = [q for q in range(19) if SPEEDS[q][2] == 1]
@@ -73,7 +73,7 @@
 
     dens_in = pltpu.make_async_copy(dens_hbm, E.at[pl.ds(5, 8), pl.ds(8, 16)], dsem)
     dens_in.start()
-    pops_in = pltpu.make_async_copy(pops_hbm, PV, psem)
+    pops_in = pltpu.make_async_copy(pops_hbm, PV.at[pl.ds(0, 19)], psem)
     pops_in.start()
 
     def remote(src, dst, send, recv, where):
@@ -482,11 +482,11 @@
             scratch_shapes=[
                 vmem(18, 32, L), vmem(14, 32, L), vmem(16, 32, L), vmem(14, 32, L),
                 vmem(256, L), vmem(256, L), vmem(12, 16, L),
-                vmem(n * 8, 128), vmem(n * 8, 128), vmem(n * 8, 128), vmem(n * 8, 128),
-                vmem(256, L), vmem(2, 2, 16, L), vmem(19, 4, 2, 2 * L),
-                vmem(2, FIELDS, 24, L), vmem(2, 18, 2, L), vmem(2, 18, 2, L),
-                vmem(2, 18, 4, L), vmem(2, 18, 4, L), vmem(2, 20, L), vmem(2, 20, L),
-                vmem(2, 80, L), vmem(19, 2, 24, L),
+                vmem(n * 8 + 8, 128), vmem(n * 8 + 8, 128), vmem(n * 8 + 8, 128), vmem(n * 8 + 8, 128),
+                vmem(256, L), vmem(3, 2, 16, L), vmem(20, 4, 2, 2 * L),
+                vmem(2, FIELDS, 24, L), vmem(3, 18, 2, L), vmem(3, 18, 2, L),
+                vmem(3, 18, 4, L), vmem(3, 18, 4, L), vmem(3, 20, L), vmem(3, 20, L),
+                vmem(2, 80, L), vmem(20, 2, 24, L),
                 dma(), dma(),
                 dma(10), dma(10), dma(8), dma(8),
                 dma(2), dma(2), dma(2), dma(2), dma(2), dma(2),

time: 35.7 us -> 35.7 us (level)
  no operation moved by 1% of the time
where the time goes in v8:
time: 35.7 us; the launch traced here: 35.6 us
  Pallas kernels  35 us (98%)
  between operations  0.64 us (2%)
    pallas_call x1, Pallas kernels, local(): pl.pallas_call(lambda *refs: kernel(nx, n, *refs), out_shape=shapes, in_s...  34.3 us

profile of v8, /device:TPU:1, one launch (start us, length us, event | category | flops | bytes accessed | tf_op | source)
XLA Modules:
  0.0 35.6 jit_solution(4353211514575255941)
XLA Ops:
  0.6 34.3 %shard_map.41 = (f32[8,16,128]{2,1,0:T(8,128)S(1)}, f32[19,4,2,256]{3,2,1,0:T(2,128)S(1)}) custom-call(f32[8,16,128]{2,1,0:T(8,128)} %refs_0_.1, f32[19,4,2,256]{3,2,1,0:T(2,128)} %refs_1_.1), custom_call_target="tpu_custom_call" | custom-call | tf_op jit(solution)/shard_map/pallas_call | solution.py:477
  34.9 0.7 %shard_map.42 = (f32[8,16,128]{2,1,0:T(8,128)}, f32[19,4,2,256]{3,2,1,0:T(2,128)}) custom-call(f32[8,16,128]{2,1,0:T(8,128)S(1)} %get-tuple-element.4.dens, f32[19,4,2,256]{3,2,1,0:T(2,128)S(1)} %get-tuple-element.5.pops), custom_call_target="tpu_custom_call" | custom-call | tf_op jit(solution)/shard_map/pallas_call | solution.py:499
